TPU v7x, 32 devices: a whole 2x2x4 slice. The times are simulated.
32 devices in a mesh: dp: 8 (over y, x, core), tensor: 4 (over z).
Axes of the slice: x: 2, y: 2, z: 4, core: 2. Of those that a mesh axis runs over, the one named last changes fastest.
Arguments:
- saved_input: bfloat16 [2048, 6144], P('dp', 'tensor'), may hold values from -6 to 6
- queries: bfloat16 [2048, 1024], P('dp', 'tensor'), may hold values from -8 to 8
- keys: bfloat16 [2048, 1024], P('dp', 'tensor'), may hold values from -8 to 8
- value_weight: bfloat16 [6144, 1024], P(None, 'tensor'), may hold values from -0.109375 to 0.109375
- grad_attended: bfloat16 [2048, 1024], P('dp', 'tensor'), may hold values from -6 to 6
Outputs:
- grad_input: bfloat16 [2048, 6144], P('dp', 'tensor')
- grad_value_weight: float32 [6144, 1024], P('dp', 'tensor')
- grad_queries: bfloat16 [2048, 1024], P('dp', 'tensor')
- grad_keys: bfloat16 [2048, 1024], P('dp', 'tensor')
All inputs are finite; a program needn't handle non-finite values.
Results may differ from a plain program's by a relative error of at most 0.02.
Values may be sent and summed in bfloat16 or wider, within the bound.
No kernel may reach another device: no remote copies, remote signals or barrier semaphores. Data moves between devices by JAX's collectives and lax.ppermute only.
A program may use at most 64 MiB of HBM per device.

v0:
```python
import jax
import jax.numpy as jnp
from jax import lax
from jax.experimental import pallas as pl
from jax.sharding import PartitionSpec as P


HD = 128
F32 = jnp.float32
BF16 = jnp.bfloat16


def dot(a, b, ca, cb):
    return lax.dot_general(a, b, (((ca,), (cb,)), ((), ())), preferred_element_type=F32)


def head_cols(h):
    return slice(h * HD, (h + 1) * HD)


def probs_kernel(q_ref, k_ref, g_ref, att_ref, gv_ref):
    tokens, width = q_ref.shape
    scale = 1.0 / jnp.sqrt(F32(HD))
    rows = lax.broadcasted_iota(jnp.int32, (tokens, tokens), 0)
    cols = lax.broadcasted_iota(jnp.int32, (tokens, tokens), 1)
    causal = rows >= cols
    for h in range(width // HD):
        c = head_cols(h)
        scores = jnp.where(causal, dot(q_ref[:, c], k_ref[:, c], 1, 1) * scale, -jnp.inf)
        e = jnp.exp(scores - jnp.max(scores, axis=-1, keepdims=True))
        att = e / jnp.sum(e, axis=-1, keepdims=True)
        att_ref[h] = att
        gv_ref[:, c] = dot(att.astype(BF16), g_ref[:, c], 0, 0).astype(BF16)


def grads_kernel(*refs):
    att_ref, q_ref, k_ref, g_ref = refs[:4]
    parts = refs[4:-2]
    dq_ref, dk_ref = refs[-2:]
    width = q_ref.shape[1]
    scale = 1.0 / jnp.sqrt(F32(HD))
    for h in range(width // HD):
        c = head_cols(h)
        v = parts[0][:, c].astype(F32)
        for part in parts[1:]:
            v = v + part[:, c].astype(F32)
        att = att_ref[h]
        gp = dot(g_ref[:, c], v.astype(BF16), 1, 1)
        row_dot = jnp.sum(att * gp, axis=-1, keepdims=True)
        gs = (att * (gp - row_dot) * scale).astype(BF16)
        dq_ref[:, c] = dot(gs, k_ref[:, c], 1, 0).astype(BF16)
        dk_ref[:, c] = dot(gs, q_ref[:, c], 0, 0).astype(BF16)


def probs_and_grad_values(q, k, g):
    tokens, width = q.shape
    return pl.pallas_call(
        probs_kernel,
        out_shape=(
            jax.ShapeDtypeStruct((width // HD, tokens, tokens), F32),
            jax.ShapeDtypeStruct((tokens, width), BF16),
        ),
        name="probs",
    )(q, k, g)


def query_key_grads(att, q, k, g, parts):
    out = jax.ShapeDtypeStruct(q.shape, BF16)
    return pl.pallas_call(grads_kernel, out_shape=(out, out), name="qk_grads")(att, q, k, g, *parts)


def pick(bit, zero, one):
    return jnp.where(bit == 0, zero, one)


def swap(x, axis, mask):
    n = lax.axis_size(axis)
    return lax.ppermute(x, axis, [(i, i ^ mask) for i in range(n)])


def by_shared_weights(saved_input, queries, keys, value_weight, grad_attended):
    nd, nt = lax.axis_size("dp"), lax.axis_size("tensor")
    d, t = lax.axis_index("dp"), lax.axis_index("tensor")
    levels = nt.bit_length() - 1
    core = d & 1
    features, width = value_weight.shape
    mine = features // nt
    half_rows, quarter, piece = mine // 2, mine // 4, mine // (2 * nd)
    bits = list(range(1, levels + 1))
    orders = (bits, bits[::-1])

    starts = []
    for half, order in enumerate(orders):
        start = half * half_rows + core * quarter
        step = quarter
        for bit in order:
            step //= 2
            start = start + ((d >> bit) & 1) * step
        starts.append(start)
    blocks = []
    for j in range(nt):
        rows = jnp.concatenate(
            [
                lax.dynamic_slice(value_weight, ((t ^ j) * mine + start, 0), (piece, width))
                for start in starts
            ],
            axis=0,
        )
        blocks.append(rows if j == 0 else swap(rows, "tensor", j))
    both = jnp.concatenate(blocks, axis=1)
    shards = [both[:piece], both[piece:]]

    def input_cols(start, size):
        return lax.dynamic_slice(saved_input, (0, start), (saved_input.shape[0], size))

    pair_input = swap(input_cols((1 - core) * half_rows, half_rows), "dp", 1)
    att, grad_values = probs_and_grad_values(queries, keys, grad_attended)
    others = [swap(grad_values, "tensor", j) for j in range(1, nt)]
    all_grads = jnp.concatenate([grad_values] + others, axis=1)

    for level in range(levels):
        for half, order in enumerate(orders):
            bit = order[levels - 1 - level]
            own = shards[half]
            other = swap(own, "dp", 1 << bit)
            b = (d >> bit) & 1
            shards[half] = jnp.concatenate([pick(b, own, other), pick(b, other, own)], axis=0)
    received = [swap(own, "dp", 1) for own in shards]

    pair_grads = swap(all_grads, "dp", 1)
    home = input_cols(core * half_rows, half_rows)
    summed = dot(home, all_grads, 0, 0)
    summed = summed + dot(pair_input, pair_grads, 0, 0)
    tiles = []
    for half, order in enumerate(orders):
        part = summed[half * quarter : (half + 1) * quarter]
        columns = {j: part[:, j * width : (j + 1) * width] for j in range(nt)}
        flip = (nt - 1) if half else 0
        chunks = {p: columns[p ^ flip] for p in range(nt)}
        for bit in order:
            b = (d >> bit) & 1
            mask = 1 << (bit - 1)
            lows = sorted(p for p in chunks if not p & mask)
            give = jnp.concatenate([pick(b, chunks[p | mask], chunks[p]) for p in lows], axis=1)
            got = swap(give.astype(BF16), "dp", 1 << bit).astype(F32)
            chunks = {
                p: pick(b, chunks[p], chunks[p | mask]) + got[:, i * width : (i + 1) * width]
                for i, p in enumerate(lows)
            }
        (tile,) = chunks.values()
        route = []
        for di in range(nd):
            for ti in range(nt):
                to = (2 * ti + (di & 1)) * nt + ((di >> 1) ^ ti ^ flip)
                route.append((di * nt + ti, to))
        tiles.append(lax.ppermute(tile.astype(BF16), ("dp", "tensor"), route))
    grad_value_weight = jnp.concatenate(tiles, axis=0).astype(F32) / F32(nd)

    own_starts = [half * half_rows + core * quarter for half in range(2)]
    pair_starts = [half * half_rows + (1 - core) * quarter for half in range(2)]
    partial = sum(dot(input_cols(s, quarter), w, 1, 0) for s, w in zip(own_starts, shards))
    partial += sum(dot(input_cols(s, quarter), w, 1, 0) for s, w in zip(pair_starts, received))
    parts = []
    for j in range(nt):
        block = partial[:, j * width : (j + 1) * width]
        parts.append(block if j == 0 else swap(block.astype(BF16), "tensor", j))
    grad_queries, grad_keys = query_key_grads(att, queries, keys, grad_attended, parts)

    pieces = []
    for own_w, pair_w in zip(shards, received):
        own = dot(all_grads, own_w, 1, 1).astype(BF16)
        pair = dot(all_grads, pair_w, 1, 1).astype(BF16)
        pieces += [pick(core, own, pair), pick(core, pair, own)]
    grad_input = jnp.concatenate(pieces, axis=1)
    return grad_input, grad_value_weight, grad_queries, grad_keys


def by_collectives(saved_input, queries, keys, value_weight, grad_attended):
    full_input = lax.all_gather(saved_input, "tensor", axis=1, tiled=True)
    att, grad_values = probs_and_grad_values(queries, keys, grad_attended)
    weight_part = dot(full_input, grad_values, 0, 0).astype(BF16)
    summed = lax.psum_scatter(weight_part, "dp", scatter_dimension=0, tiled=True).astype(F32)
    input_part = dot(grad_values, value_weight, 1, 1).astype(BF16)
    grad_input = lax.psum_scatter(input_part, "tensor", scatter_dimension=1, tiled=True)
    values = dot(full_input, value_weight, 1, 0)
    grad_queries, grad_keys = query_key_grads(att, queries, keys, grad_attended, [values])
    return grad_input, summed / F32(lax.axis_size("dp")), grad_queries, grad_keys


def solution(mesh):
    nd, nt = mesh.shape["dp"], mesh.shape["tensor"]

    def on_device(saved_input, *rest):
        paired = nd == 2 * nt and nt > 1 and nt & (nt - 1) == 0
        if paired and saved_input.shape[1] % (32 * nd) == 0:
            return by_shared_weights(saved_input, *rest)
        return by_collectives(saved_input, *rest)

    split = P("dp", "tensor")
    return jax.shard_map(
        on_device,
        mesh=mesh,
        in_specs=(split, split, split, P(None, "tensor"), split),
        out_specs=(split, split, split, split),
        check_vma=False,
    )
```

profile of v0, /device:TPU:0, one launch (start us, length us, event | category | flops | bytes accessed | tf_op | source)
XLA Modules:
  0.0 99.3 jit_solution(13105124982593042071)
XLA Ops:
  0.6 2.8 %probs.1 = (f32[2,256,256]{2,1,0:T(8,128)}, bf16[256,256]{1,0:T(8,128)(2,1)}) custom-call(bf16[256,256]{1,0:T(8,128)(2,1)} %refs_1_.1, bf16[256,256]{1,0:T(8,128)(2,1)} %refs_2_.1, bf16[256,256]{1,0:T(8,128)(2,1)} %refs_3_.1), custom_call_target="tpu_custom_call" | custom-call | tf_op jit(solution)/shard_map/probs/pallas_call | solution.py:57
  3.5 5.1 %collective-permute-start.2 = (bf16[256,256]{1,0:T(8,128)(2,1)}, bf16[256,256]{1,0:T(8,128)(2,1)S(1)}, u32[]{:S(2)}, u32[]{:S(2)}) collective-permute-start(bf16[256,256]{1,0:T(8,128)(2,1)} %get-tuple-element.8), channel_id=1, source_target_pairs={{0,3},{1,2},{2,1},{3,0},{4,7},{5,6},{6,5},{7,4},{8,11},{9,10},{10,... | collective-permute-start | bytes 393224 | tf_op jit(solution)/shard_map/ppermute | solution.py:78
  8.5 1.0 constant_dynamic-slice_fusion.8
  9.6 2.0 %collective-permute-start.5 = (bf16[192,256]{1,0:T(8,128)(2,1)S(1)}, bf16[192,256]{1,0:T(8,128)(2,1)S(1)}, u32[]{:S(2)}, u32[]{:S(2)}) collective-permute-start(bf16[192,256]{1,0:T(8,128)(2,1)S(1)} %pad_maximum_fusion.10), channel_id=1, source_target_pairs={{0,3},{1,2},{2,1},{3,0},{4,7},{5,6},{6,5},{7,4},{8,11},{9,10},{10,... | collective-permute-start | bytes 294920 | tf_op jit(solution)/shard_map/ppermute | solution.py:78
  11.5 1.6 %collective-permute-start.3 = (bf16[192,256]{1,0:T(8,128)(2,1)S(1)}, bf16[192,256]{1,0:T(8,128)(2,1)S(1)}, u32[]{:S(2)}, u32[]{:S(2)}) collective-permute-start(bf16[192,256]{1,0:T(8,128)(2,1)S(1)} %pad_maximum_fusion.8), channel_id=1, source_target_pairs={{0,1},{1,0},{2,3},{3,2},{4,5},{5,4},{6,7},{7,6},{8,9},{9,8},{10,11... | collective-permute-start | bytes 294920 | tf_op jit(solution)/shard_map/ppermute | solution.py:78
  13.2 1.0 collective-permute-start.4
  14.2 4.0 %collective-permute-done.5 = bf16[192,256]{1,0:T(8,128)(2,1)S(1)} collective-permute-done((bf16[192,256]{1,0:T(8,128)(2,1)S(1)}, bf16[192,256]{1,0:T(8,128)(2,1)S(1)}, u32[]{:S(2)}, u32[]{:S(2)}) %collective-permute-start.5) | collective-permute-done | bytes 98336 | tf_op jit(solution)/shard_map/ppermute | solution.py:78
  18.1 9.6 %collective-permute-start = (bf16[256,256]{1,0:T(8,128)(2,1)S(1)}, bf16[256,256]{1,0:T(8,128)(2,1)S(1)}, u32[]{:S(2)}, u32[]{:S(2)}) collective-permute-start(bf16[256,256]{1,0:T(8,128)(2,1)S(1)} %copy-done.4), channel_id=1, source_target_pairs={{0,1},{1,0},{2,3},{3,2},{4,5},{5,4},{6,7},{7,6},{8,9},{9,8},{10,11... | collective-permute-start | bytes 393224 | tf_op jit(solution)/shard_map/ppermute | solution.py:78
  27.7 0.6 collective-permute-done.4
  28.4 1.6 %collective-permute-start.6 = (bf16[96,1024]{1,0:T(8,128)(2,1)S(1)}, bf16[96,1024]{1,0:T(8,128)(2,1)}, u32[]{:S(2)}, u32[]{:S(2)}) collective-permute-start(bf16[96,1024]{1,0:T(8,128)(2,1)S(1)} %get-tuple-element.48), channel_id=1, source_target_pairs={{0,16},{4,20},{8,24},{12,28},{16,0},{20,4},{24,8},{28,12},{1,17},{... | collective-permute-start | bytes 589832 | tf_op jit(solution)/shard_map/ppermute | solution.py:78
  30.0 1.5 %collective-permute-start.9 = (bf16[96,1024]{1,0:T(8,128)(2,1)S(1)}, bf16[96,1024]{1,0:T(8,128)(2,1)}, u32[]{:S(2)}, u32[]{:S(2)}) collective-permute-start(bf16[96,1024]{1,0:T(8,128)(2,1)S(1)} %get-tuple-element.49), channel_id=1, source_target_pairs={{0,8},{4,12},{8,0},{12,4},{16,24},{20,28},{24,16},{28,20},{1,9},{5... | collective-permute-start | bytes 589832 | tf_op jit(solution)/shard_map/ppermute | solution.py:78
  31.7 0.5 collective-permute-start.12
  32.3 2.1 %collective-permute-done.6 = bf16[96,1024]{1,0:T(8,128)(2,1)} collective-permute-done((bf16[96,1024]{1,0:T(8,128)(2,1)S(1)}, bf16[96,1024]{1,0:T(8,128)(2,1)}, u32[]{:S(2)}, u32[]{:S(2)}) %collective-permute-start.6) | collective-permute-done | bytes 196640 | tf_op jit(solution)/shard_map/ppermute | solution.py:78
  34.4 1.4 %collective-permute-done.9 = bf16[96,1024]{1,0:T(8,128)(2,1)} collective-permute-done((bf16[96,1024]{1,0:T(8,128)(2,1)S(1)}, bf16[96,1024]{1,0:T(8,128)(2,1)}, u32[]{:S(2)}, u32[]{:S(2)}) %collective-permute-start.9) | collective-permute-done | bytes 196640 | tf_op jit(solution)/shard_map/ppermute | solution.py:78
  35.8 1.1 %broadcast_select_fusion.7 = (bf16[96,1024]{1,0:T(8,128)(2,1)S(1)}, bf16[96,1024]{1,0:T(8,128)(2,1)S(1)}, bf16[96,1024]{1,0:T(8,128)(2,1)S(1)}, bf16[96,1024]{1,0:T(8,128)(2,1)S(1)}) fusion(bf16[96,1024]{1,0:T(8,128)(2,1)} %collective-permute-done.6, pred[]{:T(512)S(6)} %eq.8, bf16[192,1024]{1,0:T(8,128)(2,1)S(1)} %pad_maximum_fusion.3, ...), kind=kLoop, calls=%fused_computation.43 | loop fusion | flops 393216 | bytes 1572866 | tf_op jit(solution)/shard_map/jit(_where)/select_n | solution.py:73
  36.9 0.6 collective-permute-start.10
  37.5 0.6 fusion.16
  38.1 0.6 convolution_add_fusion
  38.9 1.6 %collective-permute-start.17 = (bf16[384,512]{1,0:T(8,128)(2,1)S(1)}, bf16[384,512]{1,0:T(8,128)(2,1)S(1)}, u32[]{:S(2)}, u32[]{:S(2)}) collective-permute-start(bf16[384,512]{1,0:T(8,128)(2,1)S(1)} %pad_maximum_fusion.7), channel_id=1, source_target_pairs={{0,16},{4,20},{8,24},{12,28},{16,0},{20,4},{24,8},{28,12},{1,17},{... | collective-permute-start | bytes 1179656 | tf_op jit(solution)/shard_map/ppermute | solution.py:78
  40.5 1.6 %collective-permute-start.14 = (bf16[384,512]{1,0:T(8,128)(2,1)S(1)}, bf16[384,512]{1,0:T(8,128)(2,1)S(1)}, u32[]{:S(2)}, u32[]{:S(2)}) collective-permute-start(bf16[384,512]{1,0:T(8,128)(2,1)S(1)} %pad_maximum_fusion.6), channel_id=1, source_target_pairs={{0,8},{4,12},{8,0},{12,4},{16,24},{20,28},{24,16},{28,20},{1,9},{5... | collective-permute-start | bytes 1179656 | tf_op jit(solution)/shard_map/ppermute | solution.py:78
  42.1 0.6 collective-permute-start.7
  42.7 6.3 %collective-permute-done.10 = bf16[192,1024]{1,0:T(8,128)(2,1)S(1)} collective-permute-done((bf16[192,1024]{1,0:T(8,128)(2,1)S(1)}, bf16[192,1024]{1,0:T(8,128)(2,1)S(1)}, u32[]{:S(2)}, u32[]{:S(2)}) %collective-permute-start.10) | collective-permute-done | bytes 393248 | tf_op jit(solution)/shard_map/ppermute | solution.py:78
  49.2 0.9 pad_maximum_fusion.1
  50.1 4.2 %collective-permute-done.17 = bf16[384,512]{1,0:T(8,128)(2,1)S(1)} collective-permute-done((bf16[384,512]{1,0:T(8,128)(2,1)S(1)}, bf16[384,512]{1,0:T(8,128)(2,1)S(1)}, u32[]{:S(2)}, u32[]{:S(2)}) %collective-permute-start.17) | collective-permute-done | bytes 393248 | tf_op jit(solution)/shard_map/ppermute | solution.py:78
  54.8 0.6 collective-permute-start.15
  55.4 2.6 %collective-permute-done.7 = bf16[192,1024]{1,0:T(8,128)(2,1)S(1)} collective-permute-done((bf16[192,1024]{1,0:T(8,128)(2,1)S(1)}, bf16[192,1024]{1,0:T(8,128)(2,1)S(1)}, u32[]{:S(2)}, u32[]{:S(2)}) %collective-permute-start.7) | collective-permute-done | bytes 393248 | tf_op jit(solution)/shard_map/ppermute | solution.py:78
  58.2 1.6 %collective-permute-start.18 = (bf16[384,256]{1,0:T(8,128)(2,1)S(1)}, bf16[384,256]{1,0:T(8,128)(2,1)S(1)}, u32[]{:S(2)}, u32[]{:S(2)}) collective-permute-start(bf16[384,256]{1,0:T(8,128)(2,1)S(1)} %get-tuple-element.18), channel_id=1, source_target_pairs={{0,8},{4,12},{8,0},{12,4},{16,24},{20,28},{24,16},{28,20},{1,9},{5... | collective-permute-start | bytes 589832 | tf_op jit(solution)/shard_map/ppermute | solution.py:78
  59.8 0.8 collective-permute-done.15
  60.6 0.7 collective-permute-start.16
  61.3 2.6 %collective-permute-done.18 = bf16[384,256]{1,0:T(8,128)(2,1)S(1)} collective-permute-done((bf16[384,256]{1,0:T(8,128)(2,1)S(1)}, bf16[384,256]{1,0:T(8,128)(2,1)S(1)}, u32[]{:S(2)}, u32[]{:S(2)}) %collective-permute-start.18) | collective-permute-done | bytes 196640 | tf_op jit(solution)/shard_map/ppermute | solution.py:78
  64.0 0.8 add_convert_fusion
  64.7 6.2 %collective-permute-start.19 = (bf16[384,256]{1,0:T(8,128)(2,1)}, bf16[384,256]{1,0:T(8,128)(2,1)S(1)}, u32[]{:S(2)}, u32[]{:S(2)}) collective-permute-start(bf16[384,256]{1,0:T(8,128)(2,1)} %add_convert_fusion), channel_id=1, source_target_pairs={{0,3},{1,10},{2,17},{3,24},{4,7},{5,14},{6,21},{7,28},{8,2},{9,11}... | collective-permute-start | bytes 589832 | tf_op jit(solution)/shard_map/ppermute | solution.py:156
  70.9 0.9 pad_maximum_fusion
  72.3 2.1 %collective-permute-done.19 = bf16[384,256]{1,0:T(8,128)(2,1)S(1)} collective-permute-done((bf16[384,256]{1,0:T(8,128)(2,1)}, bf16[384,256]{1,0:T(8,128)(2,1)S(1)}, u32[]{:S(2)}, u32[]{:S(2)}) %collective-permute-start.19) | collective-permute-done | bytes 196640 | tf_op jit(solution)/shard_map/ppermute | solution.py:156
  74.4 0.9 convert_multiply_fusion
  75.3 1.6 %convolution_convert_fusion = bf16[256,384]{1,0:T(8,128)(2,1)S(1)} fusion(bf16[256,1024]{1,0:T(8,128)(2,1)S(1)} %constant_dynamic-update-slice_fusion, bf16[384,1024]{1,0:T(8,128)(2,1)} %collective-permute-done.11), kind=kOutput, calls=%fused_computation.4 | convolution fusion | flops 201424896 | bytes 1507328 | tf_op jit(solution)/shard_map/dot_general | solution.py:14
  76.9 0.5 broadcast_select_fusion.9
  77.4 1.6 %convolution_convert_fusion.2 = bf16[256,384]{1,0:T(8,128)(2,1)S(1)} fusion(bf16[256,1024]{1,0:T(8,128)(2,1)S(1)} %constant_dynamic-update-slice_fusion, bf16[384,1024]{1,0:T(8,128)(2,1)} %collective-permute-done.8), kind=kOutput, calls=%fused_computation.6 | convolution fusion | flops 201424896 | bytes 1507328 | tf_op jit(solution)/shard_map/dot_general | solution.py:14
  79.5 1.6 %fusion.2 = f32[256,1024]{1,0:T(8,128)S(1)} fusion(bf16[384,1024]{1,0:T(8,128)(2,1)} %collective-permute-done.11, bf16[256,1536]{1,0:T(8,128)(2,1)S(1)} %copy-done, s32[]{:T(128)S(6)} %select_n.204), kind=kOutput, calls=%fused_computation.34 | convolution fusion | flops 201326592 | bytes 2031620 | tf_op jit(solution)/shard_map/dot_general | solution.py:14
  81.1 1.6 %convolution_add_fusion.1 = f32[256,1024]{1,0:T(8,128)S(1)} fusion(f32[256,1024]{1,0:T(8,128)S(1)} %fusion.2, bf16[384,1024]{1,0:T(8,128)(2,1)} %collective-permute-done.8, bf16[256,1536]{1,0:T(8,128)(2,1)S(1)} %copy-done, s32[]{:T(128)S(6)} %select_n.203), kind=kOutput, calls=%fused_computation.1 | convolution fusion | flops 201588736 | bytes 3080196 | tf_op jit(solution)/shard_map/dot_general | solution.py:14
  83.1 4.2 %collective-permute-start.22 = (bf16[256,256]{1,0:T(8,128)(2,1)S(1)}, bf16[256,256]{1,0:T(8,128)(2,1)S(1)}, u32[]{:S(2)}, u32[]{:S(2)}) collective-permute-start(bf16[256,256]{1,0:T(8,128)(2,1)S(1)} %get-tuple-element.41), channel_id=1, source_target_pairs={{0,3},{1,2},{2,1},{3,0},{4,7},{5,6},{6,5},{7,4},{8,11},{9,10},{10,... | collective-permute-start | bytes 393224 | tf_op jit(solution)/shard_map/ppermute | solution.py:78
  87.4 0.6 collective-permute-start.20
  88.0 0.7 slice.99.refs_4_
  88.8 0.9 pad_maximum_fusion.2
  89.7 2.0 %collective-permute-done.22.refs_7_ = bf16[256,256]{1,0:T(8,128)(2,1)S(1)} collective-permute-done((bf16[256,256]{1,0:T(8,128)(2,1)S(1)}, bf16[256,256]{1,0:T(8,128)(2,1)S(1)}, u32[]{:S(2)}, u32[]{:S(2)}) %collective-permute-start.22) | collective-permute-done | bytes 131104 | tf_op jit(solution)/shard_map/ppermute | solution.py:78
  91.7 4.2 %collective-permute-done.21.refs_6_ = bf16[256,256]{1,0:T(8,128)(2,1)S(1)} collective-permute-done((bf16[256,256]{1,0:T(8,128)(2,1)S(1)}, bf16[256,256]{1,0:T(8,128)(2,1)S(1)}, u32[]{:S(2)}, u32[]{:S(2)}) %collective-permute-start.21) | collective-permute-done | bytes 131104 | tf_op jit(solution)/shard_map/ppermute | solution.py:78
  95.9 0.6 copy-done.2
  96.6 2.8 %qk_grads.1 = (bf16[256,256]{1,0:T(8,128)(2,1)}, bf16[256,256]{1,0:T(8,128)(2,1)}) custom-call(f32[2,256,256]{2,1,0:T(8,128)} %get-tuple-element.9.refs_0_, bf16[256,256]{1,0:T(8,128)(2,1)} %refs_1_.1, bf16[256,256]{1,0:T(8,128)(2,1)} %refs_2_.1, bf16[256,256]{1,0:T(8,128)(2,1)} %refs_3_.1, f32[256,256]{1,0:T(8,128)} %slice.99.refs_4_, ...), custom_call_target="tpu_custom_call" | custom-call | tf_op jit(solution)/shard_map/qk_grads/pallas_call | solution.py:69
  (50 shorter events, 2.9 us)
Async XLA Ops:
  0.6 31.0 %copy-start = (bf16[256,1536]{1,0:T(8,128)(2,1)S(1)}, bf16[256,1536]{1,0:T(8,128)(2,1)}, u32[]{:S(2)}) copy-start(bf16[256,1536]{1,0:T(8,128)(2,1)} %param.5) | copy-start | bytes 2359300
  3.5 10.7 %copy-start.4 = (bf16[256,256]{1,0:T(8,128)(2,1)S(1)}, bf16[256,256]{1,0:T(8,128)(2,1)}, u32[]{:S(2)}) copy-start(bf16[256,256]{1,0:T(8,128)(2,1)} %get-tuple-element.8) | copy-start | bytes 393220
  3.5 28.1 %collective-permute-start.2 = (bf16[256,256]{1,0:T(8,128)(2,1)}, bf16[256,256]{1,0:T(8,128)(2,1)S(1)}, u32[]{:S(2)}, u32[]{:S(2)}) collective-permute-start(bf16[256,256]{1,0:T(8,128)(2,1)} %get-tuple-element.8), channel_id=1, source_target_pairs={{0,3},{1,2},{2,1},{3,0},{4,7},{5,6},{6,5},{7,4},{8,11},{9,10},{10,... | collective-permute-start | bytes 393224 | tf_op jit(solution)/shard_map/ppermute | solution.py:78
  8.5 23.0 %collective-permute-start.1 = (bf16[256,256]{1,0:T(8,128)(2,1)}, bf16[256,256]{1,0:T(8,128)(2,1)S(1)}, u32[]{:S(2)}, u32[]{:S(2)}) collective-permute-start(bf16[256,256]{1,0:T(8,128)(2,1)} %get-tuple-element.8), channel_id=1, source_target_pairs={{0,2},{1,3},{2,0},{3,1},{4,6},{5,7},{6,4},{7,5},{8,10},{9,11},{10,... | collective-permute-start | bytes 393224 | tf_op jit(solution)/shard_map/ppermute | solution.py:78
  9.6 8.6 %collective-permute-start.5 = (bf16[192,256]{1,0:T(8,128)(2,1)S(1)}, bf16[192,256]{1,0:T(8,128)(2,1)S(1)}, u32[]{:S(2)}, u32[]{:S(2)}) collective-permute-start(bf16[192,256]{1,0:T(8,128)(2,1)S(1)} %pad_maximum_fusion.10), channel_id=1, source_target_pairs={{0,3},{1,2},{2,1},{3,0},{4,7},{5,6},{6,5},{7,4},{8,11},{9,10},{10,... | collective-permute-start | bytes 294920 | tf_op jit(solution)/shard_map/ppermute | solution.py:78
  11.5 16.2 %collective-permute-start.3 = (bf16[192,256]{1,0:T(8,128)(2,1)S(1)}, bf16[192,256]{1,0:T(8,128)(2,1)S(1)}, u32[]{:S(2)}, u32[]{:S(2)}) collective-permute-start(bf16[192,256]{1,0:T(8,128)(2,1)S(1)} %pad_maximum_fusion.8), channel_id=1, source_target_pairs={{0,1},{1,0},{2,3},{3,2},{4,5},{5,4},{6,7},{7,6},{8,9},{9,8},{10,11... | collective-permute-start | bytes 294920 | tf_op jit(solution)/shard_map/ppermute | solution.py:78
  13.2 15.2 %collective-permute-start.4 = (bf16[192,256]{1,0:T(8,128)(2,1)S(1)}, bf16[192,256]{1,0:T(8,128)(2,1)S(1)}, u32[]{:S(2)}, u32[]{:S(2)}) collective-permute-start(bf16[192,256]{1,0:T(8,128)(2,1)S(1)} %pad_maximum_fusion.9), channel_id=1, source_target_pairs={{0,2},{1,3},{2,0},{3,1},{4,6},{5,7},{6,4},{7,5},{8,10},{9,11},{10,... | collective-permute-start | bytes 294920 | tf_op jit(solution)/shard_map/ppermute | solution.py:78
  18.1 13.4 %collective-permute-start = (bf16[256,256]{1,0:T(8,128)(2,1)S(1)}, bf16[256,256]{1,0:T(8,128)(2,1)S(1)}, u32[]{:S(2)}, u32[]{:S(2)}) collective-permute-start(bf16[256,256]{1,0:T(8,128)(2,1)S(1)} %copy-done.4), channel_id=1, source_target_pairs={{0,1},{1,0},{2,3},{3,2},{4,5},{5,4},{6,7},{7,6},{8,9},{9,8},{10,11... | collective-permute-start | bytes 393224 | tf_op jit(solution)/shard_map/ppermute | solution.py:78
  28.4 6.0 %collective-permute-start.6 = (bf16[96,1024]{1,0:T(8,128)(2,1)S(1)}, bf16[96,1024]{1,0:T(8,128)(2,1)}, u32[]{:S(2)}, u32[]{:S(2)}) collective-permute-start(bf16[96,1024]{1,0:T(8,128)(2,1)S(1)} %get-tuple-element.48), channel_id=1, source_target_pairs={{0,16},{4,20},{8,24},{12,28},{16,0},{20,4},{24,8},{28,12},{1,17},{... | collective-permute-start | bytes 589832 | tf_op jit(solution)/shard_map/ppermute | solution.py:78
  30.0 5.8 %collective-permute-start.9 = (bf16[96,1024]{1,0:T(8,128)(2,1)S(1)}, bf16[96,1024]{1,0:T(8,128)(2,1)}, u32[]{:S(2)}, u32[]{:S(2)}) collective-permute-start(bf16[96,1024]{1,0:T(8,128)(2,1)S(1)} %get-tuple-element.49), channel_id=1, source_target_pairs={{0,8},{4,12},{8,0},{12,4},{16,24},{20,28},{24,16},{28,20},{1,9},{5... | collective-permute-start | bytes 589832 | tf_op jit(solution)/shard_map/ppermute | solution.py:78
  31.6 5.9 %collective-permute-start.13 = (bf16[256,1024]{1,0:T(8,128)(2,1)S(1)}, bf16[256,1024]{1,0:T(8,128)(2,1)S(1)}, u32[]{:S(2)}, u32[]{:S(2)}) collective-permute-start(bf16[256,1024]{1,0:T(8,128)(2,1)S(1)} %constant_dynamic-update-slice_fusion), channel_id=1, source_target_pairs={{0,4},{4,0},{8,12},{12,8},{16,20},{20,16},{24,28},{28,24},{1,5},{5... | collective-permute-start | bytes 1572872 | tf_op jit(solution)/shard_map/ppermute | solution.py:78
  31.7 5.8 %collective-permute-start.12 = (bf16[256,768]{1,0:T(8,128)(2,1)S(1)}, bf16[256,768]{1,0:T(8,128)(2,1)S(1)}, u32[]{:S(2)}, u32[]{:S(2)}) collective-permute-start(bf16[256,768]{1,0:T(8,128)(2,1)S(1)} %constant_dynamic-slice_fusion), channel_id=1, source_target_pairs={{0,4},{4,0},{8,12},{12,8},{16,20},{20,16},{24,28},{28,24},{1,5},{5... | collective-permute-start | bytes 1179656 | tf_op jit(solution)/shard_map/ppermute | solution.py:78
  36.9 12.1 %collective-permute-start.10 = (bf16[192,1024]{1,0:T(8,128)(2,1)S(1)}, bf16[192,1024]{1,0:T(8,128)(2,1)S(1)}, u32[]{:S(2)}, u32[]{:S(2)}) collective-permute-start(bf16[192,1024]{1,0:T(8,128)(2,1)S(1)} %pad_maximum_fusion.5), channel_id=1, source_target_pairs={{0,16},{4,20},{8,24},{12,28},{16,0},{20,4},{24,8},{28,12},{1,17},{... | collective-permute-start | bytes 1179656 | tf_op jit(solution)/shard_map/ppermute | solution.py:78
  38.9 15.4 %collective-permute-start.17 = (bf16[384,512]{1,0:T(8,128)(2,1)S(1)}, bf16[384,512]{1,0:T(8,128)(2,1)S(1)}, u32[]{:S(2)}, u32[]{:S(2)}) collective-permute-start(bf16[384,512]{1,0:T(8,128)(2,1)S(1)} %pad_maximum_fusion.7), channel_id=1, source_target_pairs={{0,16},{4,20},{8,24},{12,28},{16,0},{20,4},{24,8},{28,12},{1,17},{... | collective-permute-start | bytes 1179656 | tf_op jit(solution)/shard_map/ppermute | solution.py:78
  40.5 13.9 %collective-permute-start.14 = (bf16[384,512]{1,0:T(8,128)(2,1)S(1)}, bf16[384,512]{1,0:T(8,128)(2,1)S(1)}, u32[]{:S(2)}, u32[]{:S(2)}) collective-permute-start(bf16[384,512]{1,0:T(8,128)(2,1)S(1)} %pad_maximum_fusion.6), channel_id=1, source_target_pairs={{0,8},{4,12},{8,0},{12,4},{16,24},{20,28},{24,16},{28,20},{1,9},{5... | collective-permute-start | bytes 1179656 | tf_op jit(solution)/shard_map/ppermute | solution.py:78
  42.1 15.9 %collective-permute-start.7 = (bf16[192,1024]{1,0:T(8,128)(2,1)S(1)}, bf16[192,1024]{1,0:T(8,128)(2,1)S(1)}, u32[]{:S(2)}, u32[]{:S(2)}) collective-permute-start(bf16[192,1024]{1,0:T(8,128)(2,1)S(1)} %pad_maximum_fusion.4), channel_id=1, source_target_pairs={{0,8},{4,12},{8,0},{12,4},{16,24},{20,28},{24,16},{28,20},{1,9},{5... | collective-permute-start | bytes 1179656 | tf_op jit(solution)/shard_map/ppermute | solution.py:78
  50.1 25.2 %collective-permute-start.11 = (bf16[384,1024]{1,0:T(8,128)(2,1)}, bf16[384,1024]{1,0:T(8,128)(2,1)}, u32[]{:S(2)}, u32[]{:S(2)}) collective-permute-start(bf16[384,1024]{1,0:T(8,128)(2,1)} %pad_maximum_fusion.1), channel_id=1, source_target_pairs={{0,4},{4,0},{8,12},{12,8},{16,20},{20,16},{24,28},{28,24},{1,5},{5... | collective-permute-start | bytes 2359304 | tf_op jit(solution)/shard_map/ppermute | solution.py:78
  54.8 5.7 %collective-permute-start.15 = (bf16[384,256]{1,0:T(8,128)(2,1)S(1)}, bf16[384,256]{1,0:T(8,128)(2,1)S(1)}, u32[]{:S(2)}, u32[]{:S(2)}) collective-permute-start(bf16[384,256]{1,0:T(8,128)(2,1)S(1)} %get-tuple-element.12), channel_id=1, source_target_pairs={{0,16},{4,20},{8,24},{12,28},{16,0},{20,4},{24,8},{28,12},{1,17},{... | collective-permute-start | bytes 589832 | tf_op jit(solution)/shard_map/ppermute | solution.py:78
  58.2 5.7 %collective-permute-start.18 = (bf16[384,256]{1,0:T(8,128)(2,1)S(1)}, bf16[384,256]{1,0:T(8,128)(2,1)S(1)}, u32[]{:S(2)}, u32[]{:S(2)}) collective-permute-start(bf16[384,256]{1,0:T(8,128)(2,1)S(1)} %get-tuple-element.18), channel_id=1, source_target_pairs={{0,8},{4,12},{8,0},{12,4},{16,24},{20,28},{24,16},{28,20},{1,9},{5... | collective-permute-start | bytes 589832 | tf_op jit(solution)/shard_map/ppermute | solution.py:78
  60.6 11.7 %collective-permute-start.16 = (bf16[384,256]{1,0:T(8,128)(2,1)S(1)}, bf16[384,256]{1,0:T(8,128)(2,1)S(1)}, u32[]{:S(2)}, u32[]{:S(2)}) collective-permute-start(bf16[384,256]{1,0:T(8,128)(2,1)S(1)} %add_convert_fusion.1), channel_id=1, source_target_pairs={{0,0},{1,9},{2,18},{3,27},{4,4},{5,13},{6,22},{7,31},{8,1},{9,8},{... | collective-permute-start | bytes 589832 | tf_op jit(solution)/shard_map/ppermute | solution.py:156
  64.7 9.7 %collective-permute-start.19 = (bf16[384,256]{1,0:T(8,128)(2,1)}, bf16[384,256]{1,0:T(8,128)(2,1)S(1)}, u32[]{:S(2)}, u32[]{:S(2)}) collective-permute-start(bf16[384,256]{1,0:T(8,128)(2,1)} %add_convert_fusion), channel_id=1, source_target_pairs={{0,3},{1,10},{2,17},{3,24},{4,7},{5,14},{6,21},{7,28},{8,2},{9,11}... | collective-permute-start | bytes 589832 | tf_op jit(solution)/shard_map/ppermute | solution.py:156
  71.9 5.6 %collective-permute-start.8 = (bf16[384,1024]{1,0:T(8,128)(2,1)}, bf16[384,1024]{1,0:T(8,128)(2,1)}, u32[]{:S(2)}, u32[]{:S(2)}) collective-permute-start(bf16[384,1024]{1,0:T(8,128)(2,1)} %pad_maximum_fusion), channel_id=1, source_target_pairs={{0,4},{4,0},{8,12},{12,8},{16,20},{20,16},{24,28},{28,24},{1,5},{5... | collective-permute-start | bytes 2359304 | tf_op jit(solution)/shard_map/ppermute | solution.py:78
  83.1 8.6 %collective-permute-start.22 = (bf16[256,256]{1,0:T(8,128)(2,1)S(1)}, bf16[256,256]{1,0:T(8,128)(2,1)S(1)}, u32[]{:S(2)}, u32[]{:S(2)}) collective-permute-start(bf16[256,256]{1,0:T(8,128)(2,1)S(1)} %get-tuple-element.41), channel_id=1, source_target_pairs={{0,3},{1,2},{2,1},{3,0},{4,7},{5,6},{6,5},{7,4},{8,11},{9,10},{10,... | collective-permute-start | bytes 393224 | tf_op jit(solution)/shard_map/ppermute | solution.py:78
  87.4 8.5 %collective-permute-start.21 = (bf16[256,256]{1,0:T(8,128)(2,1)S(1)}, bf16[256,256]{1,0:T(8,128)(2,1)S(1)}, u32[]{:S(2)}, u32[]{:S(2)}) collective-permute-start(bf16[256,256]{1,0:T(8,128)(2,1)S(1)} %get-tuple-element.42), channel_id=1, source_target_pairs={{0,2},{1,3},{2,0},{3,1},{4,6},{5,7},{6,4},{7,5},{8,10},{9,11},{10,... | collective-permute-start | bytes 393224 | tf_op jit(solution)/shard_map/ppermute | solution.py:78
  87.4 8.5 %collective-permute-start.20 = (bf16[256,256]{1,0:T(8,128)(2,1)S(1)}, bf16[256,256]{1,0:T(8,128)(2,1)S(1)}, u32[]{:S(2)}, u32[]{:S(2)}) collective-permute-start(bf16[256,256]{1,0:T(8,128)(2,1)S(1)} %get-tuple-element.43), channel_id=1, source_target_pairs={{0,1},{1,0},{2,3},{3,2},{4,5},{5,4},{6,7},{7,6},{8,9},{9,8},{10,11... | collective-permute-start | bytes 393224 | tf_op jit(solution)/shard_map/ppermute | solution.py:78
  91.7 4.2 %copy-start.1 = (bf16[256,256]{1,0:T(8,128)(2,1)}, bf16[256,256]{1,0:T(8,128)(2,1)S(1)}, u32[]{:S(2)}) copy-start(bf16[256,256]{1,0:T(8,128)(2,1)S(1)} %collective-permute-done.22.refs_7_) | copy-start | bytes 393220
  95.9 0.7 copy-start.2
  95.9 0.7 copy-start.3
where the time goes:
time: 100 us; the launch traced here: 99.3 us
  starting transfers between devices  41.1 us (41%)
  waiting for transfers between devices  32.9 us (33%)
  matrix products  9.36 us (9%)
  other arithmetic  6.85 us (7%)
  Pallas kernels  5.57 us (6%)
  local copies, waits for them, and re-layouts  2.56 us (3%)
    ppermute x21, starting transfers between devices, swap(): return lax.ppermute(x, axis, [(i, i ^ mask) for i in range(n)])  34.3 us
    ppermute x21, waiting for transfers between devices, swap(): return lax.ppermute(x, axis, [(i, i ^ mask) for i in range(n)])  30.8 us
    dot_general x10, matrix products, dot(): lax.dot_general(a, b, (((ca,), (cb,)), ((), ())), preferred_element_type=...  9.36 us
    ppermute x2, starting transfers between devices, by_shared_weights(): tiles.append(lax.ppermute(tile.astype(BF16), ('dp', 'tensor'), route))  6.87 us
    pallas_call x1, Pallas kernels, probs_and_grad_values(): pl.pallas_call(probs_kernel, out_shape=(jax.ShapeDtypeStruct((width // HD...  2.82 us
    pallas_call x1, Pallas kernels, query_key_grads(): pl.pallas_call(grads_kernel, out_shape=(out, out), name='qk_grads')  2.75 us
    ppermute x2, waiting for transfers between devices, by_shared_weights(): tiles.append(lax.ppermute(tile.astype(BF16), ('dp', 'tensor'), route))  2.09 us
  transfers between devices with their start and end apart: 23, of which 12 were waited for; matrix products, arithmetic and copies ran while one was open for 12% of the time, Pallas kernels for 0%

commit v1 on v0

--- a/solution.py
+++ b/solution.py
@@ -130,7 +130,7 @@
     pair_grads = swap(all_grads, "dp", 1)
     home = input_cols(core * half_rows, half_rows)
     summed = dot(home, all_grads, 0, 0)
-    summed = summed + dot(pair_input, pair_grads, 0, 0)
+    summed = (summed + dot(pair_input, pair_grads, 0, 0)).astype(BF16)
     tiles = []
     for half, order in enumerate(orders):
         part = summed[half * quarter : (half + 1) * quarter]
@@ -142,9 +142,10 @@
             mask = 1 << (bit - 1)
             lows = sorted(p for p in chunks if not p & mask)
             give = jnp.concatenate([pick(b, chunks[p | mask], chunks[p]) for p in lows], axis=1)
-            got = swap(give.astype(BF16), "dp", 1 << bit).astype(F32)
+            got = swap(give.astype(BF16), "dp", 1 << bit)
             chunks = {
-                p: pick(b, chunks[p], chunks[p | mask]) + got[:, i * width : (i + 1) * width]
+                p: pick(b, chunks[p], chunks[p | mask]).astype(F32)
+                + got[:, i * width : (i + 1) * width].astype(F32)
                 for i, p in enumerate(lows)
             }
         (tile,) = chunks.values()

time: 100 us -> 103 us (1.030)
  the two profiles are of different devices: /device:TPU:0 before, /device:TPU:4 now
where the time goes in v1:
time: 103 us
  waiting for transfers between devices  38.6 us (37%)
  starting transfers between devices  38.4 us (37%)
  matrix products  9.36 us (9%)
  other arithmetic  7.06 us (7%)
  Pallas kernels  5.57 us (5%)
  local copies, waits for them, and re-layouts  2.54 us (2%)
    ppermute x21, starting transfers between devices, swap(): return lax.ppermute(x, axis, [(i, i ^ mask) for i in range(n)])  32.2 us
    ppermute x21, waiting for transfers between devices, swap(): return lax.ppermute(x, axis, [(i, i ^ mask) for i in range(n)])  28.8 us
    ppermute x2, waiting for transfers between devices, by_shared_weights(): tiles.append(lax.ppermute(tile.astype(BF16), ('dp', 'tensor'), route))  9.87 us
    dot_general x10, matrix products, dot(): lax.dot_general(a, b, (((ca,), (cb,)), ((), ())), preferred_element_type=...  9.36 us
    ppermute x2, starting transfers between devices, by_shared_weights(): tiles.append(lax.ppermute(tile.astype(BF16), ('dp', 'tensor'), route))  6.26 us
    pallas_call x1, Pallas kernels, probs_and_grad_values(): pl.pallas_call(probs_kernel, out_shape=(jax.ShapeDtypeStruct((width // HD...  2.82 us
    pallas_call x1, Pallas kernels, query_key_grads(): pl.pallas_call(grads_kernel, out_shape=(out, out), name='qk_grads')  2.75 us
  transfers between devices with their start and end apart: 23, of which 14 were waited for; matrix products, arithmetic and copies ran while one was open for 12% of the time, Pallas kernels for 0%

profile of v1, /device:TPU:4, one launch (start us, length us, event | category | flops | bytes accessed | tf_op | source)
XLA Modules:
  0.0 102.5 jit_solution(14578211025135499717)
XLA Ops:
  0.6 2.8 %probs.1 = (f32[2,256,256]{2,1,0:T(8,128)}, bf16[256,256]{1,0:T(8,128)(2,1)}) custom-call(bf16[256,256]{1,0:T(8,128)(2,1)} %refs_1_.1, bf16[256,256]{1,0:T(8,128)(2,1)} %refs_2_.1, bf16[256,256]{1,0:T(8,128)(2,1)} %refs_3_.1), custom_call_target="tpu_custom_call" | custom-call | tf_op jit(solution)/shard_map/probs/pallas_call | solution.py:57
  3.5 3.6 %collective-permute-start.2 = (bf16[256,256]{1,0:T(8,128)(2,1)}, bf16[256,256]{1,0:T(8,128)(2,1)S(1)}, u32[]{:S(2)}, u32[]{:S(2)}) collective-permute-start(bf16[256,256]{1,0:T(8,128)(2,1)} %get-tuple-element.8), channel_id=1, source_target_pairs={{0,3},{1,2},{2,1},{3,0},{4,7},{5,6},{6,5},{7,4},{8,11},{9,10},{10,... | collective-permute-start | bytes 393224 | tf_op jit(solution)/shard_map/ppermute | solution.py:78
  7.1 1.0 constant_dynamic-slice_fusion.8
  8.1 2.0 %collective-permute-start.5 = (bf16[192,256]{1,0:T(8,128)(2,1)S(1)}, bf16[192,256]{1,0:T(8,128)(2,1)S(1)}, u32[]{:S(2)}, u32[]{:S(2)}) collective-permute-start(bf16[192,256]{1,0:T(8,128)(2,1)S(1)} %pad_maximum_fusion.10), channel_id=1, source_target_pairs={{0,3},{1,2},{2,1},{3,0},{4,7},{5,6},{6,5},{7,4},{8,11},{9,10},{10,... | collective-permute-start | bytes 294920 | tf_op jit(solution)/shard_map/ppermute | solution.py:78
  10.1 1.6 %collective-permute-start.3 = (bf16[192,256]{1,0:T(8,128)(2,1)S(1)}, bf16[192,256]{1,0:T(8,128)(2,1)S(1)}, u32[]{:S(2)}, u32[]{:S(2)}) collective-permute-start(bf16[192,256]{1,0:T(8,128)(2,1)S(1)} %pad_maximum_fusion.8), channel_id=1, source_target_pairs={{0,1},{1,0},{2,3},{3,2},{4,5},{5,4},{6,7},{7,6},{8,9},{9,8},{10,11... | collective-permute-start | bytes 294920 | tf_op jit(solution)/shard_map/ppermute | solution.py:78
  11.7 1.0 collective-permute-start.4
  12.7 4.1 %collective-permute-done.5 = bf16[192,256]{1,0:T(8,128)(2,1)S(1)} collective-permute-done((bf16[192,256]{1,0:T(8,128)(2,1)S(1)}, bf16[192,256]{1,0:T(8,128)(2,1)S(1)}, u32[]{:S(2)}, u32[]{:S(2)}) %collective-permute-start.5) | collective-permute-done | bytes 98336 | tf_op jit(solution)/shard_map/ppermute | solution.py:78
  16.8 9.5 %collective-permute-start = (bf16[256,256]{1,0:T(8,128)(2,1)S(1)}, bf16[256,256]{1,0:T(8,128)(2,1)S(1)}, u32[]{:S(2)}, u32[]{:S(2)}) collective-permute-start(bf16[256,256]{1,0:T(8,128)(2,1)S(1)} %copy-done.4), channel_id=1, source_target_pairs={{0,1},{1,0},{2,3},{3,2},{4,5},{5,4},{6,7},{7,6},{8,9},{9,8},{10,11... | collective-permute-start | bytes 393224 | tf_op jit(solution)/shard_map/ppermute | solution.py:78
  26.3 0.6 collective-permute-done.4
  27.0 0.6 collective-permute-start.6
  27.5 1.5 %collective-permute-start.9 = (bf16[96,1024]{1,0:T(8,128)(2,1)S(1)}, bf16[96,1024]{1,0:T(8,128)(2,1)}, u32[]{:S(2)}, u32[]{:S(2)}) collective-permute-start(bf16[96,1024]{1,0:T(8,128)(2,1)S(1)} %get-tuple-element.44), channel_id=1, source_target_pairs={{0,8},{4,12},{8,0},{12,4},{16,24},{20,28},{24,16},{28,20},{1,9},{5... | collective-permute-start | bytes 589832 | tf_op jit(solution)/shard_map/ppermute | solution.py:78
  29.5 0.5 collective-permute-start.12
  30.1 2.8 %collective-permute-done.6 = bf16[96,1024]{1,0:T(8,128)(2,1)} collective-permute-done((bf16[96,1024]{1,0:T(8,128)(2,1)S(1)}, bf16[96,1024]{1,0:T(8,128)(2,1)}, u32[]{:S(2)}, u32[]{:S(2)}) %collective-permute-start.6) | collective-permute-done | bytes 196640 | tf_op jit(solution)/shard_map/ppermute | solution.py:78
  33.3 1.1 %broadcast_select_fusion.15 = (bf16[96,1024]{1,0:T(8,128)(2,1)S(1)}, bf16[96,1024]{1,0:T(8,128)(2,1)S(1)}, bf16[96,1024]{1,0:T(8,128)(2,1)S(1)}, bf16[96,1024]{1,0:T(8,128)(2,1)S(1)}) fusion(bf16[96,1024]{1,0:T(8,128)(2,1)} %collective-permute-done.6, pred[]{:T(512)S(6)} %eq.8, bf16[192,1024]{1,0:T(8,128)(2,1)S(1)} %pad_maximum_fusion.3, ...), kind=kLoop, calls=%fused_computation.47 | loop fusion | flops 393216 | bytes 1572866 | tf_op jit(solution)/shard_map/jit(_where)/select_n | solution.py:73
  34.4 1.6 %collective-permute-start.10 = (bf16[192,1024]{1,0:T(8,128)(2,1)S(1)}, bf16[192,1024]{1,0:T(8,128)(2,1)S(1)}, u32[]{:S(2)}, u32[]{:S(2)}) collective-permute-start(bf16[192,1024]{1,0:T(8,128)(2,1)S(1)} %pad_maximum_fusion.5), channel_id=1, source_target_pairs={{0,16},{4,20},{8,24},{12,28},{16,0},{20,4},{24,8},{28,12},{1,17},{... | collective-permute-start | bytes 1179656 | tf_op jit(solution)/shard_map/ppermute | solution.py:78
  36.0 0.6 fusion.16
  36.6 0.6 add_convert_fusion
  37.4 0.6 collective-permute-start.17
  38.0 1.6 %collective-permute-start.14 = (bf16[384,512]{1,0:T(8,128)(2,1)S(1)}, bf16[384,512]{1,0:T(8,128)(2,1)S(1)}, u32[]{:S(2)}, u32[]{:S(2)}) collective-permute-start(bf16[384,512]{1,0:T(8,128)(2,1)S(1)} %pad_maximum_fusion.6), channel_id=1, source_target_pairs={{0,8},{4,12},{8,0},{12,4},{16,24},{20,28},{24,16},{28,20},{1,9},{5... | collective-permute-start | bytes 1179656 | tf_op jit(solution)/shard_map/ppermute | solution.py:78
  39.6 0.6 collective-permute-start.7
  40.1 6.3 %collective-permute-done.10 = bf16[192,1024]{1,0:T(8,128)(2,1)S(1)} collective-permute-done((bf16[192,1024]{1,0:T(8,128)(2,1)S(1)}, bf16[192,1024]{1,0:T(8,128)(2,1)S(1)}, u32[]{:S(2)}, u32[]{:S(2)}) %collective-permute-start.10) | collective-permute-done | bytes 393248 | tf_op jit(solution)/shard_map/ppermute | solution.py:78
  46.7 0.9 pad_maximum_fusion.1
  47.6 4.2 %collective-permute-done.17 = bf16[384,512]{1,0:T(8,128)(2,1)S(1)} collective-permute-done((bf16[384,512]{1,0:T(8,128)(2,1)S(1)}, bf16[384,512]{1,0:T(8,128)(2,1)S(1)}, u32[]{:S(2)}, u32[]{:S(2)}) %collective-permute-start.17) | collective-permute-done | bytes 393248 | tf_op jit(solution)/shard_map/ppermute | solution.py:78
  52.1 1.6 %collective-permute-start.15 = (bf16[384,256]{1,0:T(8,128)(2,1)S(1)}, bf16[384,256]{1,0:T(8,128)(2,1)S(1)}, u32[]{:S(2)}, u32[]{:S(2)}) collective-permute-start(bf16[384,256]{1,0:T(8,128)(2,1)S(1)} %get-tuple-element.22), channel_id=1, source_target_pairs={{0,16},{4,20},{8,24},{12,28},{16,0},{20,4},{24,8},{28,12},{1,17},{... | collective-permute-start | bytes 589832 | tf_op jit(solution)/shard_map/ppermute | solution.py:78
  53.7 1.5 %collective-permute-start.18 = (bf16[384,256]{1,0:T(8,128)(2,1)S(1)}, bf16[384,256]{1,0:T(8,128)(2,1)S(1)}, u32[]{:S(2)}, u32[]{:S(2)}) collective-permute-start(bf16[384,256]{1,0:T(8,128)(2,1)S(1)} %get-tuple-element.23), channel_id=1, source_target_pairs={{0,8},{4,12},{8,0},{12,4},{16,24},{20,28},{24,16},{28,20},{1,9},{5... | collective-permute-start | bytes 589832 | tf_op jit(solution)/shard_map/ppermute | solution.py:78
  55.2 1.3 %collective-permute-done.7 = bf16[192,1024]{1,0:T(8,128)(2,1)S(1)} collective-permute-done((bf16[192,1024]{1,0:T(8,128)(2,1)S(1)}, bf16[192,1024]{1,0:T(8,128)(2,1)S(1)}, u32[]{:S(2)}, u32[]{:S(2)}) %collective-permute-start.7) | collective-permute-done | bytes 393248 | tf_op jit(solution)/shard_map/ppermute | solution.py:78
  56.8 1.1 %collective-permute-done.15 = bf16[384,256]{1,0:T(8,128)(2,1)S(1)} collective-permute-done((bf16[384,256]{1,0:T(8,128)(2,1)S(1)}, bf16[384,256]{1,0:T(8,128)(2,1)S(1)}, u32[]{:S(2)}, u32[]{:S(2)}) %collective-permute-start.15) | collective-permute-done | bytes 196640 | tf_op jit(solution)/shard_map/ppermute | solution.py:78
  57.9 1.5 %collective-permute-done.18 = bf16[384,256]{1,0:T(8,128)(2,1)S(1)} collective-permute-done((bf16[384,256]{1,0:T(8,128)(2,1)S(1)}, bf16[384,256]{1,0:T(8,128)(2,1)S(1)}, u32[]{:S(2)}, u32[]{:S(2)}) %collective-permute-start.18) | collective-permute-done | bytes 196640 | tf_op jit(solution)/shard_map/ppermute | solution.py:78
  59.7 3.9 %collective-permute-start.16 = (bf16[384,256]{1,0:T(8,128)(2,1)S(1)}, bf16[384,256]{1,0:T(8,128)(2,1)S(1)}, u32[]{:S(2)}, u32[]{:S(2)}) collective-permute-start(bf16[384,256]{1,0:T(8,128)(2,1)S(1)} %get-tuple-element.20), channel_id=1, source_target_pairs={{0,0},{1,9},{2,18},{3,27},{4,4},{5,13},{6,22},{7,31},{8,1},{9,8},{... | collective-permute-start | bytes 589832 | tf_op jit(solution)/shard_map/ppermute | solution.py:157
  63.7 2.4 %collective-permute-start.19 = (bf16[384,256]{1,0:T(8,128)(2,1)S(1)}, bf16[384,256]{1,0:T(8,128)(2,1)}, u32[]{:S(2)}, u32[]{:S(2)}) collective-permute-start(bf16[384,256]{1,0:T(8,128)(2,1)S(1)} %get-tuple-element.21), channel_id=1, source_target_pairs={{0,3},{1,10},{2,17},{3,24},{4,7},{5,14},{6,21},{7,28},{8,2},{9,11}... | collective-permute-start | bytes 589832 | tf_op jit(solution)/shard_map/ppermute | solution.py:157
  66.0 0.9 pad_maximum_fusion
  67.4 3.8 %collective-permute-done.16 = bf16[384,256]{1,0:T(8,128)(2,1)S(1)} collective-permute-done((bf16[384,256]{1,0:T(8,128)(2,1)S(1)}, bf16[384,256]{1,0:T(8,128)(2,1)S(1)}, u32[]{:S(2)}, u32[]{:S(2)}) %collective-permute-start.16) | collective-permute-done | bytes 196640 | tf_op jit(solution)/shard_map/ppermute | solution.py:157
  71.2 6.1 %collective-permute-done.19 = bf16[384,256]{1,0:T(8,128)(2,1)} collective-permute-done((bf16[384,256]{1,0:T(8,128)(2,1)S(1)}, bf16[384,256]{1,0:T(8,128)(2,1)}, u32[]{:S(2)}, u32[]{:S(2)}) %collective-permute-start.19) | collective-permute-done | bytes 196640 | tf_op jit(solution)/shard_map/ppermute | solution.py:157
  77.3 1.9 %convert_multiply_fusion = f32[768,256]{1,0:T(8,128)} fusion(bf16[384,256]{1,0:T(8,128)(2,1)} %collective-permute-done.19, bf16[384,256]{1,0:T(8,128)(2,1)S(1)} %collective-permute-done.16), kind=kLoop, calls=%fused_computation.11 | loop fusion | flops 983040 | bytes 1179648 | tf_op jit(solution)/shard_map/div | solution.py:158
  79.1 1.6 %convolution_convert_fusion = bf16[256,384]{1,0:T(8,128)(2,1)S(1)} fusion(bf16[256,1024]{1,0:T(8,128)(2,1)S(1)} %constant_dynamic-update-slice_fusion, bf16[384,1024]{1,0:T(8,128)(2,1)} %collective-permute-done.11), kind=kOutput, calls=%fused_computation.4 | convolution fusion | flops 201424896 | bytes 1507328 | tf_op jit(solution)/shard_map/dot_general | solution.py:14
  80.7 0.5 broadcast_select_fusion.17
  81.2 1.6 %convolution_convert_fusion.2 = bf16[256,384]{1,0:T(8,128)(2,1)S(1)} fusion(bf16[256,1024]{1,0:T(8,128)(2,1)S(1)} %constant_dynamic-update-slice_fusion, bf16[384,1024]{1,0:T(8,128)(2,1)} %collective-permute-done.8), kind=kOutput, calls=%fused_computation.6 | convolution fusion | flops 201424896 | bytes 1507328 | tf_op jit(solution)/shard_map/dot_general | solution.py:14
  82.8 0.5 broadcast_select_fusion.19
  83.3 1.6 %fusion.2 = f32[256,1024]{1,0:T(8,128)S(1)} fusion(bf16[384,1024]{1,0:T(8,128)(2,1)} %collective-permute-done.11, bf16[256,1536]{1,0:T(8,128)(2,1)S(1)} %copy-done, s32[]{:T(128)S(6)} %select_n.206), kind=kOutput, calls=%fused_computation.30 | convolution fusion | flops 201326592 | bytes 2031620 | tf_op jit(solution)/shard_map/dot_general | solution.py:14
  84.9 1.6 %convolution_add_fusion = f32[256,1024]{1,0:T(8,128)S(1)} fusion(f32[256,1024]{1,0:T(8,128)S(1)} %fusion.2, bf16[384,1024]{1,0:T(8,128)(2,1)} %collective-permute-done.8, bf16[256,1536]{1,0:T(8,128)(2,1)S(1)} %copy-done, s32[]{:T(128)S(6)} %select_n.205), kind=kOutput, calls=%fused_computation.1 | convolution fusion | flops 201588736 | bytes 3080196 | tf_op jit(solution)/shard_map/dot_general | solution.py:14
  87.0 0.7 collective-permute-start.21
  87.7 3.7 %collective-permute-start.20 = (bf16[256,256]{1,0:T(8,128)(2,1)S(1)}, bf16[256,256]{1,0:T(8,128)(2,1)S(1)}, u32[]{:S(2)}, u32[]{:S(2)}) collective-permute-start(bf16[256,256]{1,0:T(8,128)(2,1)S(1)} %get-tuple-element.38), channel_id=1, source_target_pairs={{0,1},{1,0},{2,3},{3,2},{4,5},{5,4},{6,7},{7,6},{8,9},{9,8},{10,11... | collective-permute-start | bytes 393224 | tf_op jit(solution)/shard_map/ppermute | solution.py:78
  91.4 0.7 slice.99.refs_4_
  92.1 0.9 pad_maximum_fusion.2
  93.1 2.1 %collective-permute-done.22.refs_7_ = bf16[256,256]{1,0:T(8,128)(2,1)S(1)} collective-permute-done((bf16[256,256]{1,0:T(8,128)(2,1)S(1)}, bf16[256,256]{1,0:T(8,128)(2,1)S(1)}, u32[]{:S(2)}, u32[]{:S(2)}) %collective-permute-start.22) | collective-permute-done | bytes 131104 | tf_op jit(solution)/shard_map/ppermute | solution.py:78
  95.2 3.9 %collective-permute-done.21.refs_6_ = bf16[256,256]{1,0:T(8,128)(2,1)S(1)} collective-permute-done((bf16[256,256]{1,0:T(8,128)(2,1)S(1)}, bf16[256,256]{1,0:T(8,128)(2,1)S(1)}, u32[]{:S(2)}, u32[]{:S(2)}) %collective-permute-start.21) | collective-permute-done | bytes 131104 | tf_op jit(solution)/shard_map/ppermute | solution.py:78
  99.1 0.6 copy-done.2
  99.8 2.8 %qk_grads.1 = (bf16[256,256]{1,0:T(8,128)(2,1)}, bf16[256,256]{1,0:T(8,128)(2,1)}) custom-call(f32[2,256,256]{2,1,0:T(8,128)} %get-tuple-element.9.refs_0_, bf16[256,256]{1,0:T(8,128)(2,1)} %refs_1_.1, bf16[256,256]{1,0:T(8,128)(2,1)} %refs_2_.1, bf16[256,256]{1,0:T(8,128)(2,1)} %refs_3_.1, f32[256,256]{1,0:T(8,128)} %slice.99.refs_4_, ...), custom_call_target="tpu_custom_call" | custom-call | tf_op jit(solution)/shard_map/qk_grads/pallas_call | solution.py:69
  (47 shorter events, 3.2 us)
Async XLA Ops:
  0.6 28.9 %copy-start = (bf16[256,1536]{1,0:T(8,128)(2,1)S(1)}, bf16[256,1536]{1,0:T(8,128)(2,1)}, u32[]{:S(2)}) copy-start(bf16[256,1536]{1,0:T(8,128)(2,1)} %param.5) | copy-start | bytes 2359300
  3.5 9.2 %copy-start.4 = (bf16[256,256]{1,0:T(8,128)(2,1)S(1)}, bf16[256,256]{1,0:T(8,128)(2,1)}, u32[]{:S(2)}) copy-start(bf16[256,256]{1,0:T(8,128)(2,1)} %get-tuple-element.8) | copy-start | bytes 393220
  3.5 25.9 %collective-permute-start.2 = (bf16[256,256]{1,0:T(8,128)(2,1)}, bf16[256,256]{1,0:T(8,128)(2,1)S(1)}, u32[]{:S(2)}, u32[]{:S(2)}) collective-permute-start(bf16[256,256]{1,0:T(8,128)(2,1)} %get-tuple-element.8), channel_id=1, source_target_pairs={{0,3},{1,2},{2,1},{3,0},{4,7},{5,6},{6,5},{7,4},{8,11},{9,10},{10,... | collective-permute-start | bytes 393224 | tf_op jit(solution)/shard_map/ppermute | solution.py:78
  7.1 22.3 %collective-permute-start.1 = (bf16[256,256]{1,0:T(8,128)(2,1)}, bf16[256,256]{1,0:T(8,128)(2,1)S(1)}, u32[]{:S(2)}, u32[]{:S(2)}) collective-permute-start(bf16[256,256]{1,0:T(8,128)(2,1)} %get-tuple-element.8), channel_id=1, source_target_pairs={{0,2},{1,3},{2,0},{3,1},{4,6},{5,7},{6,4},{7,5},{8,10},{9,11},{10,... | collective-permute-start | bytes 393224 | tf_op jit(solution)/shard_map/ppermute | solution.py:78
  8.1 8.7 %collective-permute-start.5 = (bf16[192,256]{1,0:T(8,128)(2,1)S(1)}, bf16[192,256]{1,0:T(8,128)(2,1)S(1)}, u32[]{:S(2)}, u32[]{:S(2)}) collective-permute-start(bf16[192,256]{1,0:T(8,128)(2,1)S(1)} %pad_maximum_fusion.10), channel_id=1, source_target_pairs={{0,3},{1,2},{2,1},{3,0},{4,7},{5,6},{6,5},{7,4},{8,11},{9,10},{10,... | collective-permute-start | bytes 294920 | tf_op jit(solution)/shard_map/ppermute | solution.py:78
  10.1 16.2 %collective-permute-start.3 = (bf16[192,256]{1,0:T(8,128)(2,1)S(1)}, bf16[192,256]{1,0:T(8,128)(2,1)S(1)}, u32[]{:S(2)}, u32[]{:S(2)}) collective-permute-start(bf16[192,256]{1,0:T(8,128)(2,1)S(1)} %pad_maximum_fusion.8), channel_id=1, source_target_pairs={{0,1},{1,0},{2,3},{3,2},{4,5},{5,4},{6,7},{7,6},{8,9},{9,8},{10,11... | collective-permute-start | bytes 294920 | tf_op jit(solution)/shard_map/ppermute | solution.py:78
  11.7 15.2 %collective-permute-start.4 = (bf16[192,256]{1,0:T(8,128)(2,1)S(1)}, bf16[192,256]{1,0:T(8,128)(2,1)S(1)}, u32[]{:S(2)}, u32[]{:S(2)}) collective-permute-start(bf16[192,256]{1,0:T(8,128)(2,1)S(1)} %pad_maximum_fusion.9), channel_id=1, source_target_pairs={{0,2},{1,3},{2,0},{3,1},{4,6},{5,7},{6,4},{7,5},{8,10},{9,11},{10,... | collective-permute-start | bytes 294920 | tf_op jit(solution)/shard_map/ppermute | solution.py:78
  16.8 12.6 %collective-permute-start = (bf16[256,256]{1,0:T(8,128)(2,1)S(1)}, bf16[256,256]{1,0:T(8,128)(2,1)S(1)}, u32[]{:S(2)}, u32[]{:S(2)}) collective-permute-start(bf16[256,256]{1,0:T(8,128)(2,1)S(1)} %copy-done.4), channel_id=1, source_target_pairs={{0,1},{1,0},{2,3},{3,2},{4,5},{5,4},{6,7},{7,6},{8,9},{9,8},{10,11... | collective-permute-start | bytes 393224 | tf_op jit(solution)/shard_map/ppermute | solution.py:78
  27.0 6.0 %collective-permute-start.6 = (bf16[96,1024]{1,0:T(8,128)(2,1)S(1)}, bf16[96,1024]{1,0:T(8,128)(2,1)}, u32[]{:S(2)}, u32[]{:S(2)}) collective-permute-start(bf16[96,1024]{1,0:T(8,128)(2,1)S(1)} %get-tuple-element.43), channel_id=1, source_target_pairs={{0,16},{4,20},{8,24},{12,28},{16,0},{20,4},{24,8},{28,12},{1,17},{... | collective-permute-start | bytes 589832 | tf_op jit(solution)/shard_map/ppermute | solution.py:78
  27.5 5.8 %collective-permute-start.9 = (bf16[96,1024]{1,0:T(8,128)(2,1)S(1)}, bf16[96,1024]{1,0:T(8,128)(2,1)}, u32[]{:S(2)}, u32[]{:S(2)}) collective-permute-start(bf16[96,1024]{1,0:T(8,128)(2,1)S(1)} %get-tuple-element.44), channel_id=1, source_target_pairs={{0,8},{4,12},{8,0},{12,4},{16,24},{20,28},{24,16},{28,20},{1,9},{5... | collective-permute-start | bytes 589832 | tf_op jit(solution)/shard_map/ppermute | solution.py:78
  29.4 6.6 %collective-permute-start.13 = (bf16[256,1024]{1,0:T(8,128)(2,1)S(1)}, bf16[256,1024]{1,0:T(8,128)(2,1)S(1)}, u32[]{:S(2)}, u32[]{:S(2)}) collective-permute-start(bf16[256,1024]{1,0:T(8,128)(2,1)S(1)} %constant_dynamic-update-slice_fusion), channel_id=1, source_target_pairs={{0,4},{4,0},{8,12},{12,8},{16,20},{20,16},{24,28},{28,24},{1,5},{5... | collective-permute-start | bytes 1572872 | tf_op jit(solution)/shard_map/ppermute | solution.py:78
  29.5 6.5 %collective-permute-start.12 = (bf16[256,768]{1,0:T(8,128)(2,1)S(1)}, bf16[256,768]{1,0:T(8,128)(2,1)S(1)}, u32[]{:S(2)}, u32[]{:S(2)}) collective-permute-start(bf16[256,768]{1,0:T(8,128)(2,1)S(1)} %constant_dynamic-slice_fusion), channel_id=1, source_target_pairs={{0,4},{4,0},{8,12},{12,8},{16,20},{20,16},{24,28},{28,24},{1,5},{5... | collective-permute-start | bytes 1179656 | tf_op jit(solution)/shard_map/ppermute | solution.py:78
  34.4 12.1 %collective-permute-start.10 = (bf16[192,1024]{1,0:T(8,128)(2,1)S(1)}, bf16[192,1024]{1,0:T(8,128)(2,1)S(1)}, u32[]{:S(2)}, u32[]{:S(2)}) collective-permute-start(bf16[192,1024]{1,0:T(8,128)(2,1)S(1)} %pad_maximum_fusion.5), channel_id=1, source_target_pairs={{0,16},{4,20},{8,24},{12,28},{16,0},{20,4},{24,8},{28,12},{1,17},{... | collective-permute-start | bytes 1179656 | tf_op jit(solution)/shard_map/ppermute | solution.py:78
  37.4 14.5 %collective-permute-start.17 = (bf16[384,512]{1,0:T(8,128)(2,1)S(1)}, bf16[384,512]{1,0:T(8,128)(2,1)S(1)}, u32[]{:S(2)}, u32[]{:S(2)}) collective-permute-start(bf16[384,512]{1,0:T(8,128)(2,1)S(1)} %pad_maximum_fusion.7), channel_id=1, source_target_pairs={{0,16},{4,20},{8,24},{12,28},{16,0},{20,4},{24,8},{28,12},{1,17},{... | collective-permute-start | bytes 1179656 | tf_op jit(solution)/shard_map/ppermute | solution.py:78
  38.0 13.9 %collective-permute-start.14 = (bf16[384,512]{1,0:T(8,128)(2,1)S(1)}, bf16[384,512]{1,0:T(8,128)(2,1)S(1)}, u32[]{:S(2)}, u32[]{:S(2)}) collective-permute-start(bf16[384,512]{1,0:T(8,128)(2,1)S(1)} %pad_maximum_fusion.6), channel_id=1, source_target_pairs={{0,8},{4,12},{8,0},{12,4},{16,24},{20,28},{24,16},{28,20},{1,9},{5... | collective-permute-start | bytes 1179656 | tf_op jit(solution)/shard_map/ppermute | solution.py:78
  39.6 17.0 %collective-permute-start.7 = (bf16[192,1024]{1,0:T(8,128)(2,1)S(1)}, bf16[192,1024]{1,0:T(8,128)(2,1)S(1)}, u32[]{:S(2)}, u32[]{:S(2)}) collective-permute-start(bf16[192,1024]{1,0:T(8,128)(2,1)S(1)} %pad_maximum_fusion.4), channel_id=1, source_target_pairs={{0,8},{4,12},{8,0},{12,4},{16,24},{20,28},{24,16},{28,20},{1,9},{5... | collective-permute-start | bytes 1179656 | tf_op jit(solution)/shard_map/ppermute | solution.py:78
  47.6 31.5 %collective-permute-start.11 = (bf16[384,1024]{1,0:T(8,128)(2,1)}, bf16[384,1024]{1,0:T(8,128)(2,1)}, u32[]{:S(2)}, u32[]{:S(2)}) collective-permute-start(bf16[384,1024]{1,0:T(8,128)(2,1)} %pad_maximum_fusion.1), channel_id=1, source_target_pairs={{0,4},{4,0},{8,12},{12,8},{16,20},{20,16},{24,28},{28,24},{1,5},{5... | collective-permute-start | bytes 2359304 | tf_op jit(solution)/shard_map/ppermute | solution.py:78
  52.1 5.7 %collective-permute-start.15 = (bf16[384,256]{1,0:T(8,128)(2,1)S(1)}, bf16[384,256]{1,0:T(8,128)(2,1)S(1)}, u32[]{:S(2)}, u32[]{:S(2)}) collective-permute-start(bf16[384,256]{1,0:T(8,128)(2,1)S(1)} %get-tuple-element.22), channel_id=1, source_target_pairs={{0,16},{4,20},{8,24},{12,28},{16,0},{20,4},{24,8},{28,12},{1,17},{... | collective-permute-start | bytes 589832 | tf_op jit(solution)/shard_map/ppermute | solution.py:78
  53.7 5.7 %collective-permute-start.18 = (bf16[384,256]{1,0:T(8,128)(2,1)S(1)}, bf16[384,256]{1,0:T(8,128)(2,1)S(1)}, u32[]{:S(2)}, u32[]{:S(2)}) collective-permute-start(bf16[384,256]{1,0:T(8,128)(2,1)S(1)} %get-tuple-element.23), channel_id=1, source_target_pairs={{0,8},{4,12},{8,0},{12,4},{16,24},{20,28},{24,16},{28,20},{1,9},{5... | collective-permute-start | bytes 589832 | tf_op jit(solution)/shard_map/ppermute | solution.py:78
  59.7 11.4 %collective-permute-start.16 = (bf16[384,256]{1,0:T(8,128)(2,1)S(1)}, bf16[384,256]{1,0:T(8,128)(2,1)S(1)}, u32[]{:S(2)}, u32[]{:S(2)}) collective-permute-start(bf16[384,256]{1,0:T(8,128)(2,1)S(1)} %get-tuple-element.20), channel_id=1, source_target_pairs={{0,0},{1,9},{2,18},{3,27},{4,4},{5,13},{6,22},{7,31},{8,1},{9,8},{... | collective-permute-start | bytes 589832 | tf_op jit(solution)/shard_map/ppermute | solution.py:157
  63.7 13.6 %collective-permute-start.19 = (bf16[384,256]{1,0:T(8,128)(2,1)S(1)}, bf16[384,256]{1,0:T(8,128)(2,1)}, u32[]{:S(2)}, u32[]{:S(2)}) collective-permute-start(bf16[384,256]{1,0:T(8,128)(2,1)S(1)} %get-tuple-element.21), channel_id=1, source_target_pairs={{0,3},{1,10},{2,17},{3,24},{4,7},{5,14},{6,21},{7,28},{8,2},{9,11}... | collective-permute-start | bytes 589832 | tf_op jit(solution)/shard_map/ppermute | solution.py:157
  67.0 14.2 %collective-permute-start.8 = (bf16[384,1024]{1,0:T(8,128)(2,1)}, bf16[384,1024]{1,0:T(8,128)(2,1)}, u32[]{:S(2)}, u32[]{:S(2)}) collective-permute-start(bf16[384,1024]{1,0:T(8,128)(2,1)} %pad_maximum_fusion), channel_id=1, source_target_pairs={{0,4},{4,0},{8,12},{12,8},{16,20},{20,16},{24,28},{28,24},{1,5},{5... | collective-permute-start | bytes 2359304 | tf_op jit(solution)/shard_map/ppermute | solution.py:78
  86.9 8.2 %collective-permute-start.22 = (bf16[256,256]{1,0:T(8,128)(2,1)S(1)}, bf16[256,256]{1,0:T(8,128)(2,1)S(1)}, u32[]{:S(2)}, u32[]{:S(2)}) collective-permute-start(bf16[256,256]{1,0:T(8,128)(2,1)S(1)} %get-tuple-element.36), channel_id=1, source_target_pairs={{0,3},{1,2},{2,1},{3,0},{4,7},{5,6},{6,5},{7,4},{8,11},{9,10},{10,... | collective-permute-start | bytes 393224 | tf_op jit(solution)/shard_map/ppermute | solution.py:78
  87.0 12.0 %collective-permute-start.21 = (bf16[256,256]{1,0:T(8,128)(2,1)S(1)}, bf16[256,256]{1,0:T(8,128)(2,1)S(1)}, u32[]{:S(2)}, u32[]{:S(2)}) collective-permute-start(bf16[256,256]{1,0:T(8,128)(2,1)S(1)} %get-tuple-element.37), channel_id=1, source_target_pairs={{0,2},{1,3},{2,0},{3,1},{4,6},{5,7},{6,4},{7,5},{8,10},{9,11},{10,... | collective-permute-start | bytes 393224 | tf_op jit(solution)/shard_map/ppermute | solution.py:78
  87.7 11.4 %collective-permute-start.20 = (bf16[256,256]{1,0:T(8,128)(2,1)S(1)}, bf16[256,256]{1,0:T(8,128)(2,1)S(1)}, u32[]{:S(2)}, u32[]{:S(2)}) collective-permute-start(bf16[256,256]{1,0:T(8,128)(2,1)S(1)} %get-tuple-element.38), channel_id=1, source_target_pairs={{0,1},{1,0},{2,3},{3,2},{4,5},{5,4},{6,7},{7,6},{8,9},{9,8},{10,11... | collective-permute-start | bytes 393224 | tf_op jit(solution)/shard_map/ppermute | solution.py:78
  95.2 3.9 %copy-start.1 = (bf16[256,256]{1,0:T(8,128)(2,1)}, bf16[256,256]{1,0:T(8,128)(2,1)S(1)}, u32[]{:S(2)}) copy-start(bf16[256,256]{1,0:T(8,128)(2,1)S(1)} %collective-permute-done.22.refs_7_) | copy-start | bytes 393220
  99.1 0.6 copy-start.2
  99.1 0.7 copy-start.3

commit v2 on v1

--- a/solution.py
+++ b/solution.py
@@ -142,10 +142,10 @@
             mask = 1 << (bit - 1)
             lows = sorted(p for p in chunks if not p & mask)
             give = jnp.concatenate([pick(b, chunks[p | mask], chunks[p]) for p in lows], axis=1)
-            got = swap(give.astype(BF16), "dp", 1 << bit)
+            got = swap(give.astype(BF16), "dp", 1 << bit).astype(F32)
             chunks = {
                 p: pick(b, chunks[p], chunks[p | mask]).astype(F32)
-                + got[:, i * width : (i + 1) * width].astype(F32)
+                + got[:, i * width : (i + 1) * width]
                 for i, p in enumerate(lows)
             }
         (tile,) = chunks.values()
@@ -161,10 +161,11 @@
     pair_starts = [half * half_rows + (1 - core) * quarter for half in range(2)]
     partial = sum(dot(input_cols(s, quarter), w, 1, 0) for s, w in zip(own_starts, shards))
     partial += sum(dot(input_cols(s, quarter), w, 1, 0) for s, w in zip(pair_starts, received))
+    partial = partial.astype(BF16)
     parts = []
     for j in range(nt):
         block = partial[:, j * width : (j + 1) * width]
-        parts.append(block if j == 0 else swap(block.astype(BF16), "tensor", j))
+        parts.append(block if j == 0 else swap(block, "tensor", j))
     grad_queries, grad_keys = query_key_grads(att, queries, keys, grad_attended, parts)
 
     pieces = []

time: 103 us -> 103 us (level)
  no operation moved by 1% of the time
where the time goes in v2:
time: 103 us
  waiting for transfers between devices  39 us (38%)
  starting transfers between devices  38.3 us (37%)
  matrix products  9.36 us (9%)
  other arithmetic  7.14 us (7%)
  Pallas kernels  5.53 us (5%)
  local copies, waits for them, and re-layouts  2.51 us (2%)
    ppermute x21, starting transfers between devices, swap(): return lax.ppermute(x, axis, [(i, i ^ mask) for i in range(n)])  32.1 us
    ppermute x21, waiting for transfers between devices, swap(): return lax.ppermute(x, axis, [(i, i ^ mask) for i in range(n)])  29.3 us
    ppermute x2, waiting for transfers between devices, by_shared_weights(): tiles.append(lax.ppermute(tile.astype(BF16), ('dp', 'tensor'), route))  9.74 us
    dot_general x10, matrix products, dot(): lax.dot_general(a, b, (((ca,), (cb,)), ((), ())), preferred_element_type=...  9.36 us
    ppermute x2, starting transfers between devices, by_shared_weights(): tiles.append(lax.ppermute(tile.astype(BF16), ('dp', 'tensor'), route))  6.14 us
    pallas_call x1, Pallas kernels, probs_and_grad_values(): pl.pallas_call(probs_kernel, out_shape=(jax.ShapeDtypeStruct((width // HD...  2.82 us
    pallas_call x1, Pallas kernels, query_key_grads(): pl.pallas_call(grads_kernel, out_shape=(out, out), name='qk_grads')  2.71 us
  transfers between devices with their start and end apart: 23, of which 14 were waited for; matrix products, arithmetic and copies ran while one was open for 12% of the time, Pallas kernels for 0%

profile of v2, /device:TPU:4, one launch (start us, length us, event | category | flops | bytes accessed | tf_op | source)
XLA Modules:
  0.0 102.7 jit_solution(7002045846231465999)
XLA Ops:
  0.6 2.8 %probs.1 = (f32[2,256,256]{2,1,0:T(8,128)}, bf16[256,256]{1,0:T(8,128)(2,1)}) custom-call(bf16[256,256]{1,0:T(8,128)(2,1)} %refs_1_.1, bf16[256,256]{1,0:T(8,128)(2,1)} %refs_2_.1, bf16[256,256]{1,0:T(8,128)(2,1)} %refs_3_.1), custom_call_target="tpu_custom_call" | custom-call | tf_op jit(solution)/shard_map/probs/pallas_call | solution.py:57
  3.5 3.6 %collective-permute-start.2 = (bf16[256,256]{1,0:T(8,128)(2,1)}, bf16[256,256]{1,0:T(8,128)(2,1)S(1)}, u32[]{:S(2)}, u32[]{:S(2)}) collective-permute-start(bf16[256,256]{1,0:T(8,128)(2,1)} %get-tuple-element.8), channel_id=1, source_target_pairs={{0,3},{1,2},{2,1},{3,0},{4,7},{5,6},{6,5},{7,4},{8,11},{9,10},{10,... | collective-permute-start | bytes 393224 | tf_op jit(solution)/shard_map/ppermute | solution.py:78
  7.1 1.0 constant_dynamic-slice_fusion.8
  8.1 2.0 %collective-permute-start.5 = (bf16[192,256]{1,0:T(8,128)(2,1)S(1)}, bf16[192,256]{1,0:T(8,128)(2,1)S(1)}, u32[]{:S(2)}, u32[]{:S(2)}) collective-permute-start(bf16[192,256]{1,0:T(8,128)(2,1)S(1)} %pad_maximum_fusion.10), channel_id=1, source_target_pairs={{0,3},{1,2},{2,1},{3,0},{4,7},{5,6},{6,5},{7,4},{8,11},{9,10},{10,... | collective-permute-start | bytes 294920 | tf_op jit(solution)/shard_map/ppermute | solution.py:78
  10.1 1.6 %collective-permute-start.3 = (bf16[192,256]{1,0:T(8,128)(2,1)S(1)}, bf16[192,256]{1,0:T(8,128)(2,1)S(1)}, u32[]{:S(2)}, u32[]{:S(2)}) collective-permute-start(bf16[192,256]{1,0:T(8,128)(2,1)S(1)} %pad_maximum_fusion.8), channel_id=1, source_target_pairs={{0,1},{1,0},{2,3},{3,2},{4,5},{5,4},{6,7},{7,6},{8,9},{9,8},{10,11... | collective-permute-start | bytes 294920 | tf_op jit(solution)/shard_map/ppermute | solution.py:78
  11.7 1.0 collective-permute-start.4
  12.7 4.1 %collective-permute-done.5 = bf16[192,256]{1,0:T(8,128)(2,1)S(1)} collective-permute-done((bf16[192,256]{1,0:T(8,128)(2,1)S(1)}, bf16[192,256]{1,0:T(8,128)(2,1)S(1)}, u32[]{:S(2)}, u32[]{:S(2)}) %collective-permute-start.5) | collective-permute-done | bytes 98336 | tf_op jit(solution)/shard_map/ppermute | solution.py:78
  16.8 9.5 %collective-permute-start = (bf16[256,256]{1,0:T(8,128)(2,1)S(1)}, bf16[256,256]{1,0:T(8,128)(2,1)S(1)}, u32[]{:S(2)}, u32[]{:S(2)}) collective-permute-start(bf16[256,256]{1,0:T(8,128)(2,1)S(1)} %copy-done.1), channel_id=1, source_target_pairs={{0,1},{1,0},{2,3},{3,2},{4,5},{5,4},{6,7},{7,6},{8,9},{9,8},{10,11... | collective-permute-start | bytes 393224 | tf_op jit(solution)/shard_map/ppermute | solution.py:78
  26.3 0.6 collective-permute-done.4
  27.0 0.6 collective-permute-start.6
  27.5 1.5 %collective-permute-start.9 = (bf16[96,1024]{1,0:T(8,128)(2,1)S(1)}, bf16[96,1024]{1,0:T(8,128)(2,1)}, u32[]{:S(2)}, u32[]{:S(2)}) collective-permute-start(bf16[96,1024]{1,0:T(8,128)(2,1)S(1)} %get-tuple-element.45), channel_id=1, source_target_pairs={{0,8},{4,12},{8,0},{12,4},{16,24},{20,28},{24,16},{28,20},{1,9},{5... | collective-permute-start | bytes 589832 | tf_op jit(solution)/shard_map/ppermute | solution.py:78
  29.5 0.5 collective-permute-start.12
  30.1 2.8 %collective-permute-done.6 = bf16[96,1024]{1,0:T(8,128)(2,1)} collective-permute-done((bf16[96,1024]{1,0:T(8,128)(2,1)S(1)}, bf16[96,1024]{1,0:T(8,128)(2,1)}, u32[]{:S(2)}, u32[]{:S(2)}) %collective-permute-start.6) | collective-permute-done | bytes 196640 | tf_op jit(solution)/shard_map/ppermute | solution.py:78
  33.3 1.1 %broadcast_select_fusion.15 = (bf16[96,1024]{1,0:T(8,128)(2,1)S(1)}, bf16[96,1024]{1,0:T(8,128)(2,1)S(1)}, bf16[96,1024]{1,0:T(8,128)(2,1)S(1)}, bf16[96,1024]{1,0:T(8,128)(2,1)S(1)}) fusion(bf16[96,1024]{1,0:T(8,128)(2,1)} %collective-permute-done.6, pred[]{:T(512)S(6)} %eq.8, bf16[192,1024]{1,0:T(8,128)(2,1)S(1)} %pad_maximum_fusion.3, ...), kind=kLoop, calls=%fused_computation.48 | loop fusion | flops 393216 | bytes 1572866 | tf_op jit(solution)/shard_map/jit(_where)/select_n | solution.py:73
  34.4 1.6 %collective-permute-start.10 = (bf16[192,1024]{1,0:T(8,128)(2,1)S(1)}, bf16[192,1024]{1,0:T(8,128)(2,1)S(1)}, u32[]{:S(2)}, u32[]{:S(2)}) collective-permute-start(bf16[192,1024]{1,0:T(8,128)(2,1)S(1)} %pad_maximum_fusion.5), channel_id=1, source_target_pairs={{0,16},{4,20},{8,24},{12,28},{16,0},{20,4},{24,8},{28,12},{1,17},{... | collective-permute-start | bytes 1179656 | tf_op jit(solution)/shard_map/ppermute | solution.py:78
  36.0 0.6 fusion.16
  36.6 0.6 add_convert_fusion
  37.4 0.6 collective-permute-start.17
  38.0 1.6 %collective-permute-start.14 = (bf16[384,512]{1,0:T(8,128)(2,1)S(1)}, bf16[384,512]{1,0:T(8,128)(2,1)S(1)}, u32[]{:S(2)}, u32[]{:S(2)}) collective-permute-start(bf16[384,512]{1,0:T(8,128)(2,1)S(1)} %pad_maximum_fusion.6), channel_id=1, source_target_pairs={{0,8},{4,12},{8,0},{12,4},{16,24},{20,28},{24,16},{28,20},{1,9},{5... | collective-permute-start | bytes 1179656 | tf_op jit(solution)/shard_map/ppermute | solution.py:78
  39.6 0.6 collective-permute-start.7
  40.1 6.3 %collective-permute-done.10 = bf16[192,1024]{1,0:T(8,128)(2,1)S(1)} collective-permute-done((bf16[192,1024]{1,0:T(8,128)(2,1)S(1)}, bf16[192,1024]{1,0:T(8,128)(2,1)S(1)}, u32[]{:S(2)}, u32[]{:S(2)}) %collective-permute-start.10) | collective-permute-done | bytes 393248 | tf_op jit(solution)/shard_map/ppermute | solution.py:78
  46.7 0.9 pad_maximum_fusion.1
  47.6 4.2 %collective-permute-done.17 = bf16[384,512]{1,0:T(8,128)(2,1)S(1)} collective-permute-done((bf16[384,512]{1,0:T(8,128)(2,1)S(1)}, bf16[384,512]{1,0:T(8,128)(2,1)S(1)}, u32[]{:S(2)}, u32[]{:S(2)}) %collective-permute-start.17) | collective-permute-done | bytes 393248 | tf_op jit(solution)/shard_map/ppermute | solution.py:78
  52.3 1.6 %collective-permute-start.15 = (bf16[384,256]{1,0:T(8,128)(2,1)S(1)}, bf16[384,256]{1,0:T(8,128)(2,1)S(1)}, u32[]{:S(2)}, u32[]{:S(2)}) collective-permute-start(bf16[384,256]{1,0:T(8,128)(2,1)S(1)} %get-tuple-element.22), channel_id=1, source_target_pairs={{0,16},{4,20},{8,24},{12,28},{16,0},{20,4},{24,8},{28,12},{1,17},{... | collective-permute-start | bytes 589832 | tf_op jit(solution)/shard_map/ppermute | solution.py:78
  53.8 1.5 %collective-permute-start.18 = (bf16[384,256]{1,0:T(8,128)(2,1)S(1)}, bf16[384,256]{1,0:T(8,128)(2,1)S(1)}, u32[]{:S(2)}, u32[]{:S(2)}) collective-permute-start(bf16[384,256]{1,0:T(8,128)(2,1)S(1)} %get-tuple-element.23), channel_id=1, source_target_pairs={{0,8},{4,12},{8,0},{12,4},{16,24},{20,28},{24,16},{28,20},{1,9},{5... | collective-permute-start | bytes 589832 | tf_op jit(solution)/shard_map/ppermute | solution.py:78
  55.3 1.1 %collective-permute-done.7 = bf16[192,1024]{1,0:T(8,128)(2,1)S(1)} collective-permute-done((bf16[192,1024]{1,0:T(8,128)(2,1)S(1)}, bf16[192,1024]{1,0:T(8,128)(2,1)S(1)}, u32[]{:S(2)}, u32[]{:S(2)}) %collective-permute-start.7) | collective-permute-done | bytes 393248 | tf_op jit(solution)/shard_map/ppermute | solution.py:78
  56.6 1.4 %collective-permute-done.15 = bf16[384,256]{1,0:T(8,128)(2,1)S(1)} collective-permute-done((bf16[384,256]{1,0:T(8,128)(2,1)S(1)}, bf16[384,256]{1,0:T(8,128)(2,1)S(1)}, u32[]{:S(2)}, u32[]{:S(2)}) %collective-permute-start.15) | collective-permute-done | bytes 196640 | tf_op jit(solution)/shard_map/ppermute | solution.py:78
  58.0 1.5 %collective-permute-done.18 = bf16[384,256]{1,0:T(8,128)(2,1)S(1)} collective-permute-done((bf16[384,256]{1,0:T(8,128)(2,1)S(1)}, bf16[384,256]{1,0:T(8,128)(2,1)S(1)}, u32[]{:S(2)}, u32[]{:S(2)}) %collective-permute-start.18) | collective-permute-done | bytes 196640 | tf_op jit(solution)/shard_map/ppermute | solution.py:78
  59.8 3.8 %collective-permute-start.16 = (bf16[384,256]{1,0:T(8,128)(2,1)S(1)}, bf16[384,256]{1,0:T(8,128)(2,1)S(1)}, u32[]{:S(2)}, u32[]{:S(2)}) collective-permute-start(bf16[384,256]{1,0:T(8,128)(2,1)S(1)} %get-tuple-element.20), channel_id=1, source_target_pairs={{0,0},{1,9},{2,18},{3,27},{4,4},{5,13},{6,22},{7,31},{8,1},{9,8},{... | collective-permute-start | bytes 589832 | tf_op jit(solution)/shard_map/ppermute | solution.py:157
  63.6 2.4 %collective-permute-start.19 = (bf16[384,256]{1,0:T(8,128)(2,1)S(1)}, bf16[384,256]{1,0:T(8,128)(2,1)}, u32[]{:S(2)}, u32[]{:S(2)}) collective-permute-start(bf16[384,256]{1,0:T(8,128)(2,1)S(1)} %get-tuple-element.21), channel_id=1, source_target_pairs={{0,3},{1,10},{2,17},{3,24},{4,7},{5,14},{6,21},{7,28},{8,2},{9,11}... | collective-permute-start | bytes 589832 | tf_op jit(solution)/shard_map/ppermute | solution.py:157
  66.0 0.9 pad_maximum_fusion
  67.4 3.8 %collective-permute-done.16 = bf16[384,256]{1,0:T(8,128)(2,1)S(1)} collective-permute-done((bf16[384,256]{1,0:T(8,128)(2,1)S(1)}, bf16[384,256]{1,0:T(8,128)(2,1)S(1)}, u32[]{:S(2)}, u32[]{:S(2)}) %collective-permute-start.16) | collective-permute-done | bytes 196640 | tf_op jit(solution)/shard_map/ppermute | solution.py:157
  71.1 6.0 %collective-permute-done.19 = bf16[384,256]{1,0:T(8,128)(2,1)} collective-permute-done((bf16[384,256]{1,0:T(8,128)(2,1)S(1)}, bf16[384,256]{1,0:T(8,128)(2,1)}, u32[]{:S(2)}, u32[]{:S(2)}) %collective-permute-start.19) | collective-permute-done | bytes 196640 | tf_op jit(solution)/shard_map/ppermute | solution.py:157
  77.1 1.9 %convert_multiply_fusion = f32[768,256]{1,0:T(8,128)} fusion(bf16[384,256]{1,0:T(8,128)(2,1)} %collective-permute-done.19, bf16[384,256]{1,0:T(8,128)(2,1)S(1)} %collective-permute-done.16), kind=kLoop, calls=%fused_computation.12 | loop fusion | flops 983040 | bytes 1179648 | tf_op jit(solution)/shard_map/div | solution.py:158
  79.0 1.6 %convolution_convert_fusion = bf16[256,384]{1,0:T(8,128)(2,1)S(1)} fusion(bf16[256,1024]{1,0:T(8,128)(2,1)S(1)} %constant_dynamic-update-slice_fusion, bf16[384,1024]{1,0:T(8,128)(2,1)} %collective-permute-done.11), kind=kOutput, calls=%fused_computation.5 | convolution fusion | flops 201424896 | bytes 1507328 | tf_op jit(solution)/shard_map/dot_general | solution.py:14
  80.6 0.5 broadcast_select_fusion.17
  81.0 1.6 %convolution_convert_fusion.2 = bf16[256,384]{1,0:T(8,128)(2,1)S(1)} fusion(bf16[256,1024]{1,0:T(8,128)(2,1)S(1)} %constant_dynamic-update-slice_fusion, bf16[384,1024]{1,0:T(8,128)(2,1)} %collective-permute-done.8), kind=kOutput, calls=%fused_computation.7 | convolution fusion | flops 201424896 | bytes 1507328 | tf_op jit(solution)/shard_map/dot_general | solution.py:14
  82.6 0.5 broadcast_select_fusion.19
  83.1 1.6 %fusion.3 = f32[256,1024]{1,0:T(8,128)S(1)} fusion(bf16[384,1024]{1,0:T(8,128)(2,1)} %collective-permute-done.11, bf16[256,1536]{1,0:T(8,128)(2,1)S(1)} %copy-done, s32[]{:T(128)S(6)} %select_n.206), kind=kOutput, calls=%fused_computation.31 | convolution fusion | flops 201326592 | bytes 2031620 | tf_op jit(solution)/shard_map/dot_general | solution.py:14
  84.7 1.6 %convolution_add_fusion = f32[256,1024]{1,0:T(8,128)S(1)} fusion(f32[256,1024]{1,0:T(8,128)S(1)} %fusion.3, bf16[384,1024]{1,0:T(8,128)(2,1)} %collective-permute-done.8, bf16[256,1536]{1,0:T(8,128)(2,1)S(1)} %copy-done, s32[]{:T(128)S(6)} %select_n.205), kind=kOutput, calls=%fused_computation.1 | convolution fusion | flops 201588736 | bytes 3080196 | tf_op jit(solution)/shard_map/dot_general | solution.py:14
  86.7 0.7 fusion.14
  87.4 1.0 collective-permute-start.21
  88.4 3.4 %collective-permute-start.20 = (bf16[256,256]{1,0:T(8,128)(2,1)S(1)}, bf16[256,256]{1,0:T(8,128)(2,1)S(1)}, u32[]{:S(2)}, u32[]{:S(2)}) collective-permute-start(bf16[256,256]{1,0:T(8,128)(2,1)S(1)} %get-tuple-element.38), channel_id=1, source_target_pairs={{0,1},{1,0},{2,3},{3,2},{4,5},{5,4},{6,7},{7,6},{8,9},{9,8},{10,11... | collective-permute-start | bytes 393224 | tf_op jit(solution)/shard_map/ppermute | solution.py:78
  91.8 0.9 pad_maximum_fusion.2
  92.8 2.8 %collective-permute-done.22.refs_7_ = bf16[256,256]{1,0:T(8,128)(2,1)S(1)} collective-permute-done((bf16[256,256]{1,0:T(8,128)(2,1)S(1)}, bf16[256,256]{1,0:T(8,128)(2,1)S(1)}, u32[]{:S(2)}, u32[]{:S(2)}) %collective-permute-start.22) | collective-permute-done | bytes 131104 | tf_op jit(solution)/shard_map/ppermute | solution.py:78
  95.6 3.7 %collective-permute-done.21.refs_6_ = bf16[256,256]{1,0:T(8,128)(2,1)S(1)} collective-permute-done((bf16[256,256]{1,0:T(8,128)(2,1)S(1)}, bf16[256,256]{1,0:T(8,128)(2,1)S(1)}, u32[]{:S(2)}, u32[]{:S(2)}) %collective-permute-start.21) | collective-permute-done | bytes 131104 | tf_op jit(solution)/shard_map/ppermute | solution.py:78
  99.3 0.6 copy-done.3
  100.0 2.7 %qk_grads.1 = (bf16[256,256]{1,0:T(8,128)(2,1)}, bf16[256,256]{1,0:T(8,128)(2,1)}) custom-call(f32[2,256,256]{2,1,0:T(8,128)} %get-tuple-element.9.refs_0_, bf16[256,256]{1,0:T(8,128)(2,1)} %refs_1_.1, bf16[256,256]{1,0:T(8,128)(2,1)} %refs_2_.1, bf16[256,256]{1,0:T(8,128)(2,1)} %refs_3_.1, bf16[256,256]{1,0:T(8,128)(2,1)} %get-tuple-element.39.refs_4_, ...), custom_call_target="tpu_custom_call" | custom-call | tf_op jit(solution)/shard_map/qk_grads/pallas_call | solution.py:69
  (48 shorter events, 3.2 us)
Async XLA Ops:
  0.6 28.9 %copy-start = (bf16[256,1536]{1,0:T(8,128)(2,1)S(1)}, bf16[256,1536]{1,0:T(8,128)(2,1)}, u32[]{:S(2)}) copy-start(bf16[256,1536]{1,0:T(8,128)(2,1)} %param.5) | copy-start | bytes 2359300
  3.5 9.2 %copy-start.1 = (bf16[256,256]{1,0:T(8,128)(2,1)S(1)}, bf16[256,256]{1,0:T(8,128)(2,1)}, u32[]{:S(2)}) copy-start(bf16[256,256]{1,0:T(8,128)(2,1)} %get-tuple-element.8) | copy-start | bytes 393220
  3.5 25.9 %collective-permute-start.2 = (bf16[256,256]{1,0:T(8,128)(2,1)}, bf16[256,256]{1,0:T(8,128)(2,1)S(1)}, u32[]{:S(2)}, u32[]{:S(2)}) collective-permute-start(bf16[256,256]{1,0:T(8,128)(2,1)} %get-tuple-element.8), channel_id=1, source_target_pairs={{0,3},{1,2},{2,1},{3,0},{4,7},{5,6},{6,5},{7,4},{8,11},{9,10},{10,... | collective-permute-start | bytes 393224 | tf_op jit(solution)/shard_map/ppermute | solution.py:78
  7.1 22.3 %collective-permute-start.1 = (bf16[256,256]{1,0:T(8,128)(2,1)}, bf16[256,256]{1,0:T(8,128)(2,1)S(1)}, u32[]{:S(2)}, u32[]{:S(2)}) collective-permute-start(bf16[256,256]{1,0:T(8,128)(2,1)} %get-tuple-element.8), channel_id=1, source_target_pairs={{0,2},{1,3},{2,0},{3,1},{4,6},{5,7},{6,4},{7,5},{8,10},{9,11},{10,... | collective-permute-start | bytes 393224 | tf_op jit(solution)/shard_map/ppermute | solution.py:78
  8.1 8.7 %collective-permute-start.5 = (bf16[192,256]{1,0:T(8,128)(2,1)S(1)}, bf16[192,256]{1,0:T(8,128)(2,1)S(1)}, u32[]{:S(2)}, u32[]{:S(2)}) collective-permute-start(bf16[192,256]{1,0:T(8,128)(2,1)S(1)} %pad_maximum_fusion.10), channel_id=1, source_target_pairs={{0,3},{1,2},{2,1},{3,0},{4,7},{5,6},{6,5},{7,4},{8,11},{9,10},{10,... | collective-permute-start | bytes 294920 | tf_op jit(solution)/shard_map/ppermute | solution.py:78
  10.1 16.2 %collective-permute-start.3 = (bf16[192,256]{1,0:T(8,128)(2,1)S(1)}, bf16[192,256]{1,0:T(8,128)(2,1)S(1)}, u32[]{:S(2)}, u32[]{:S(2)}) collective-permute-start(bf16[192,256]{1,0:T(8,128)(2,1)S(1)} %pad_maximum_fusion.8), channel_id=1, source_target_pairs={{0,1},{1,0},{2,3},{3,2},{4,5},{5,4},{6,7},{7,6},{8,9},{9,8},{10,11... | collective-permute-start | bytes 294920 | tf_op jit(solution)/shard_map/ppermute | solution.py:78
  11.7 15.2 %collective-permute-start.4 = (bf16[192,256]{1,0:T(8,128)(2,1)S(1)}, bf16[192,256]{1,0:T(8,128)(2,1)S(1)}, u32[]{:S(2)}, u32[]{:S(2)}) collective-permute-start(bf16[192,256]{1,0:T(8,128)(2,1)S(1)} %pad_maximum_fusion.9), channel_id=1, source_target_pairs={{0,2},{1,3},{2,0},{3,1},{4,6},{5,7},{6,4},{7,5},{8,10},{9,11},{10,... | collective-permute-start | bytes 294920 | tf_op jit(solution)/shard_map/ppermute | solution.py:78
  16.8 12.6 %collective-permute-start = (bf16[256,256]{1,0:T(8,128)(2,1)S(1)}, bf16[256,256]{1,0:T(8,128)(2,1)S(1)}, u32[]{:S(2)}, u32[]{:S(2)}) collective-permute-start(bf16[256,256]{1,0:T(8,128)(2,1)S(1)} %copy-done.1), channel_id=1, source_target_pairs={{0,1},{1,0},{2,3},{3,2},{4,5},{5,4},{6,7},{7,6},{8,9},{9,8},{10,11... | collective-permute-start | bytes 393224 | tf_op jit(solution)/shard_map/ppermute | solution.py:78
  27.0 6.0 %collective-permute-start.6 = (bf16[96,1024]{1,0:T(8,128)(2,1)S(1)}, bf16[96,1024]{1,0:T(8,128)(2,1)}, u32[]{:S(2)}, u32[]{:S(2)}) collective-permute-start(bf16[96,1024]{1,0:T(8,128)(2,1)S(1)} %get-tuple-element.44), channel_id=1, source_target_pairs={{0,16},{4,20},{8,24},{12,28},{16,0},{20,4},{24,8},{28,12},{1,17},{... | collective-permute-start | bytes 589832 | tf_op jit(solution)/shard_map/ppermute | solution.py:78
  27.5 5.8 %collective-permute-start.9 = (bf16[96,1024]{1,0:T(8,128)(2,1)S(1)}, bf16[96,1024]{1,0:T(8,128)(2,1)}, u32[]{:S(2)}, u32[]{:S(2)}) collective-permute-start(bf16[96,1024]{1,0:T(8,128)(2,1)S(1)} %get-tuple-element.45), channel_id=1, source_target_pairs={{0,8},{4,12},{8,0},{12,4},{16,24},{20,28},{24,16},{28,20},{1,9},{5... | collective-permute-start | bytes 589832 | tf_op jit(solution)/shard_map/ppermute | solution.py:78
  29.4 6.6 %collective-permute-start.13 = (bf16[256,1024]{1,0:T(8,128)(2,1)S(1)}, bf16[256,1024]{1,0:T(8,128)(2,1)S(1)}, u32[]{:S(2)}, u32[]{:S(2)}) collective-permute-start(bf16[256,1024]{1,0:T(8,128)(2,1)S(1)} %constant_dynamic-update-slice_fusion), channel_id=1, source_target_pairs={{0,4},{4,0},{8,12},{12,8},{16,20},{20,16},{24,28},{28,24},{1,5},{5... | collective-permute-start | bytes 1572872 | tf_op jit(solution)/shard_map/ppermute | solution.py:78
  29.5 6.5 %collective-permute-start.12 = (bf16[256,768]{1,0:T(8,128)(2,1)S(1)}, bf16[256,768]{1,0:T(8,128)(2,1)S(1)}, u32[]{:S(2)}, u32[]{:S(2)}) collective-permute-start(bf16[256,768]{1,0:T(8,128)(2,1)S(1)} %constant_dynamic-slice_fusion), channel_id=1, source_target_pairs={{0,4},{4,0},{8,12},{12,8},{16,20},{20,16},{24,28},{28,24},{1,5},{5... | collective-permute-start | bytes 1179656 | tf_op jit(solution)/shard_map/ppermute | solution.py:78
  34.4 12.1 %collective-permute-start.10 = (bf16[192,1024]{1,0:T(8,128)(2,1)S(1)}, bf16[192,1024]{1,0:T(8,128)(2,1)S(1)}, u32[]{:S(2)}, u32[]{:S(2)}) collective-permute-start(bf16[192,1024]{1,0:T(8,128)(2,1)S(1)} %pad_maximum_fusion.5), channel_id=1, source_target_pairs={{0,16},{4,20},{8,24},{12,28},{16,0},{20,4},{24,8},{28,12},{1,17},{... | collective-permute-start | bytes 1179656 | tf_op jit(solution)/shard_map/ppermute | solution.py:78
  37.4 14.4 %collective-permute-start.17 = (bf16[384,512]{1,0:T(8,128)(2,1)S(1)}, bf16[384,512]{1,0:T(8,128)(2,1)S(1)}, u32[]{:S(2)}, u32[]{:S(2)}) collective-permute-start(bf16[384,512]{1,0:T(8,128)(2,1)S(1)} %pad_maximum_fusion.7), channel_id=1, source_target_pairs={{0,16},{4,20},{8,24},{12,28},{16,0},{20,4},{24,8},{28,12},{1,17},{... | collective-permute-start | bytes 1179656 | tf_op jit(solution)/shard_map/ppermute | solution.py:78
  38.0 13.9 %collective-permute-start.14 = (bf16[384,512]{1,0:T(8,128)(2,1)S(1)}, bf16[384,512]{1,0:T(8,128)(2,1)S(1)}, u32[]{:S(2)}, u32[]{:S(2)}) collective-permute-start(bf16[384,512]{1,0:T(8,128)(2,1)S(1)} %pad_maximum_fusion.6), channel_id=1, source_target_pairs={{0,8},{4,12},{8,0},{12,4},{16,24},{20,28},{24,16},{28,20},{1,9},{5... | collective-permute-start | bytes 1179656 | tf_op jit(solution)/shard_map/ppermute | solution.py:78
  39.6 16.9 %collective-permute-start.7 = (bf16[192,1024]{1,0:T(8,128)(2,1)S(1)}, bf16[192,1024]{1,0:T(8,128)(2,1)S(1)}, u32[]{:S(2)}, u32[]{:S(2)}) collective-permute-start(bf16[192,1024]{1,0:T(8,128)(2,1)S(1)} %pad_maximum_fusion.4), channel_id=1, source_target_pairs={{0,8},{4,12},{8,0},{12,4},{16,24},{20,28},{24,16},{28,20},{1,9},{5... | collective-permute-start | bytes 1179656 | tf_op jit(solution)/shard_map/ppermute | solution.py:78
  47.6 31.3 %collective-permute-start.11 = (bf16[384,1024]{1,0:T(8,128)(2,1)}, bf16[384,1024]{1,0:T(8,128)(2,1)}, u32[]{:S(2)}, u32[]{:S(2)}) collective-permute-start(bf16[384,1024]{1,0:T(8,128)(2,1)} %pad_maximum_fusion.1), channel_id=1, source_target_pairs={{0,4},{4,0},{8,12},{12,8},{16,20},{20,16},{24,28},{28,24},{1,5},{5... | collective-permute-start | bytes 2359304 | tf_op jit(solution)/shard_map/ppermute | solution.py:78
  52.3 5.7 %collective-permute-start.15 = (bf16[384,256]{1,0:T(8,128)(2,1)S(1)}, bf16[384,256]{1,0:T(8,128)(2,1)S(1)}, u32[]{:S(2)}, u32[]{:S(2)}) collective-permute-start(bf16[384,256]{1,0:T(8,128)(2,1)S(1)} %get-tuple-element.22), channel_id=1, source_target_pairs={{0,16},{4,20},{8,24},{12,28},{16,0},{20,4},{24,8},{28,12},{1,17},{... | collective-permute-start | bytes 589832 | tf_op jit(solution)/shard_map/ppermute | solution.py:78
  53.8 5.7 %collective-permute-start.18 = (bf16[384,256]{1,0:T(8,128)(2,1)S(1)}, bf16[384,256]{1,0:T(8,128)(2,1)S(1)}, u32[]{:S(2)}, u32[]{:S(2)}) collective-permute-start(bf16[384,256]{1,0:T(8,128)(2,1)S(1)} %get-tuple-element.23), channel_id=1, source_target_pairs={{0,8},{4,12},{8,0},{12,4},{16,24},{20,28},{24,16},{28,20},{1,9},{5... | collective-permute-start | bytes 589832 | tf_op jit(solution)/shard_map/ppermute | solution.py:78
  59.8 11.3 %collective-permute-start.16 = (bf16[384,256]{1,0:T(8,128)(2,1)S(1)}, bf16[384,256]{1,0:T(8,128)(2,1)S(1)}, u32[]{:S(2)}, u32[]{:S(2)}) collective-permute-start(bf16[384,256]{1,0:T(8,128)(2,1)S(1)} %get-tuple-element.20), channel_id=1, source_target_pairs={{0,0},{1,9},{2,18},{3,27},{4,4},{5,13},{6,22},{7,31},{8,1},{9,8},{... | collective-permute-start | bytes 589832 | tf_op jit(solution)/shard_map/ppermute | solution.py:157
  63.6 13.5 %collective-permute-start.19 = (bf16[384,256]{1,0:T(8,128)(2,1)S(1)}, bf16[384,256]{1,0:T(8,128)(2,1)}, u32[]{:S(2)}, u32[]{:S(2)}) collective-permute-start(bf16[384,256]{1,0:T(8,128)(2,1)S(1)} %get-tuple-element.21), channel_id=1, source_target_pairs={{0,3},{1,10},{2,17},{3,24},{4,7},{5,14},{6,21},{7,28},{8,2},{9,11}... | collective-permute-start | bytes 589832 | tf_op jit(solution)/shard_map/ppermute | solution.py:157
  66.9 14.1 %collective-permute-start.8 = (bf16[384,1024]{1,0:T(8,128)(2,1)}, bf16[384,1024]{1,0:T(8,128)(2,1)}, u32[]{:S(2)}, u32[]{:S(2)}) collective-permute-start(bf16[384,1024]{1,0:T(8,128)(2,1)} %pad_maximum_fusion), channel_id=1, source_target_pairs={{0,4},{4,0},{8,12},{12,8},{16,20},{20,16},{24,28},{28,24},{1,5},{5... | collective-permute-start | bytes 2359304 | tf_op jit(solution)/shard_map/ppermute | solution.py:78
  87.4 8.2 %collective-permute-start.22 = (bf16[256,256]{1,0:T(8,128)(2,1)S(1)}, bf16[256,256]{1,0:T(8,128)(2,1)S(1)}, u32[]{:S(2)}, u32[]{:S(2)}) collective-permute-start(bf16[256,256]{1,0:T(8,128)(2,1)S(1)} %get-tuple-element.36), channel_id=1, source_target_pairs={{0,3},{1,2},{2,1},{3,0},{4,7},{5,6},{6,5},{7,4},{8,11},{9,10},{10,... | collective-permute-start | bytes 393224 | tf_op jit(solution)/shard_map/ppermute | solution.py:78
  87.4 11.9 %collective-permute-start.21 = (bf16[256,256]{1,0:T(8,128)(2,1)S(1)}, bf16[256,256]{1,0:T(8,128)(2,1)S(1)}, u32[]{:S(2)}, u32[]{:S(2)}) collective-permute-start(bf16[256,256]{1,0:T(8,128)(2,1)S(1)} %get-tuple-element.37), channel_id=1, source_target_pairs={{0,2},{1,3},{2,0},{3,1},{4,6},{5,7},{6,4},{7,5},{8,10},{9,11},{10,... | collective-permute-start | bytes 393224 | tf_op jit(solution)/shard_map/ppermute | solution.py:78
  88.4 10.9 %collective-permute-start.20 = (bf16[256,256]{1,0:T(8,128)(2,1)S(1)}, bf16[256,256]{1,0:T(8,128)(2,1)S(1)}, u32[]{:S(2)}, u32[]{:S(2)}) collective-permute-start(bf16[256,256]{1,0:T(8,128)(2,1)S(1)} %get-tuple-element.38), channel_id=1, source_target_pairs={{0,1},{1,0},{2,3},{3,2},{4,5},{5,4},{6,7},{7,6},{8,9},{9,8},{10,11... | collective-permute-start | bytes 393224 | tf_op jit(solution)/shard_map/ppermute | solution.py:78
  95.6 3.7 %copy-start.2 = (bf16[256,256]{1,0:T(8,128)(2,1)}, bf16[256,256]{1,0:T(8,128)(2,1)S(1)}, u32[]{:S(2)}) copy-start(bf16[256,256]{1,0:T(8,128)(2,1)S(1)} %collective-permute-done.22.refs_7_) | copy-start | bytes 393220
  99.3 0.7 copy-start.3
  99.3 0.7 copy-start.4
